TPU v7x, 32 devices: a whole 2x2x4 slice. The times are simulated.
32 devices in a mesh: group: 2 (over x), blk: 16 (over z, y, core).
Axes of the slice: x: 2, y: 2, z: 4, core: 2. Of those that a mesh axis runs over, the one named last changes fastest.
Arguments:
- spectra: bfloat16 [2, 2048, 768], P(None, ('group', 'blk')), parts along dimension 1, may hold values from -6 to 6
- gap_mask: int32 [2048, 48], P(('group', 'blk')), parts along dimension 0, may hold values 0 or 1
Outputs:
- correlation: float32 [8, 2048, 1024], P(None, ('group', 'blk')), parts along dimension 1
There are 2 independent parts, one for each index of `group`. A program takes and returns all parts, laid end to end along the dimension named above; each array names one. Nothing has to cross between parts.
All inputs are finite; a program needn't handle non-finite values. No bound on the sum of `gap_mask` on one device may be relied on, other than what follows from the above.
Results may differ from a plain program's by a relative error of at most 0.0085.
Values may be sent and summed in bfloat16 or wider, within the bound.
No kernel may reach another device: no remote copies, remote signals or barrier semaphores. Data moves between devices by JAX's collectives and lax.ppermute only.
A program may use at most 192 MiB of HBM per device.

v0:
```python
import math

import numpy as np
import jax
import jax.numpy as jnp
from jax import lax
from jax.experimental import pallas as pl
from jax.experimental.pallas import tpu as pltpu
from jax.sharding import PartitionSpec as P


LAGS = 8

level_floor = 0.3
first_bin = 96.0
REACH = 2
ROOM = 16 * 2**20
PARTS = 2


def phase_tables(bin_count, win_count, lag_count):
    freq = first_bin + np.arange(bin_count, dtype=np.float64)
    shifts = 3.0 + 5.0 * np.arange(lag_count, dtype=np.float64)
    theta = 2.0 * math.pi * shifts[:, None] * freq[None, :] / 512.0
    scale = 1.0 / math.sqrt(win_count * bin_count)
    tables = [np.tile(part(theta) * scale, (1, win_count)) for part in (np.cos, np.sin)]
    return [jnp.asarray(t[:, None, :], jnp.float32) for t in tables]


def near(array):
    return pltpu.with_memory_space_constraint(array, pltpu.VMEM)


def far(array):
    return pltpu.with_memory_space_constraint(array, pltpu.HBM)


def whiten_body(spectra, gap_mask, out):
    wide = spectra.shape[2]
    bin_count = wide // gap_mask.shape[0]
    real = spectra[0].astype(jnp.float32)
    imag = spectra[1].astype(jnp.float32)
    amplitude = jnp.sqrt(real * real + imag * imag)
    lane = lax.broadcasted_iota(jnp.int32, amplitude.shape, 1) % bin_count
    total = amplitude
    count = jnp.ones(amplitude.shape, jnp.float32)
    for step in range(1, REACH + 1):
        above = lane + step < bin_count
        below = lane >= step
        total = total + jnp.where(above, pltpu.roll(amplitude, wide - step, 1), 0.0)
        total = total + jnp.where(below, pltpu.roll(amplitude, step, 1), 0.0)
        count = count + above.astype(jnp.float32) + below.astype(jnp.float32)
    level = jnp.maximum(total / count, level_floor)
    window = lax.broadcasted_iota(jnp.int32, (gap_mask.shape[0], wide), 1) // bin_count
    spread = window == lax.broadcasted_iota(jnp.int32, window.shape, 0)
    kept = lax.dot_general(
        gap_mask[...].astype(jnp.float32).astype(jnp.bfloat16),
        spread.astype(jnp.float32).astype(jnp.bfloat16),
        (((0,), (0,)), ((), ())),
        preferred_element_type=jnp.float32,
    )
    factor = kept / level
    out[:, :wide] = (real * factor).astype(jnp.bfloat16)
    out[:, wide:] = (imag * factor).astype(jnp.bfloat16)


def whiten(spectra, gap_mask):
    members, wide = spectra.shape[1:]
    return pl.pallas_call(
        whiten_body,
        out_shape=pltpu.VMEM((members, 2 * wide), jnp.bfloat16),
        compiler_params=pltpu.CompilerParams(vmem_limit_bytes=ROOM),
        name="whiten",
    )(far(spectra), far(gap_mask.T))


def modulate_body(white, cosine, sine, out):
    members = white.shape[0]
    wide = white.shape[1] // 2
    real = white[:, :wide].astype(jnp.float32)
    imag = white[:, wide:].astype(jnp.float32)
    for lag in range(cosine.shape[0]):
        rows = slice(lag * members, (lag + 1) * members)
        c = cosine[lag]
        s = sine[lag]
        out[rows, :wide] = (c * real - s * imag).astype(jnp.bfloat16)
        out[rows, wide:] = (c * imag + s * real).astype(jnp.bfloat16)


def modulate(white, win_count):
    members = white.shape[0]
    cosine, sine = phase_tables(white.shape[1] // 2 // win_count, win_count, LAGS)
    return pl.pallas_call(
        modulate_body,
        out_shape=pltpu.VMEM((LAGS * members, white.shape[1]), jnp.bfloat16),
        compiler_params=pltpu.CompilerParams(vmem_limit_bytes=ROOM),
        cost_estimate=pl.CostEstimate(flops=12 * LAGS * white.size, bytes_accessed=0, transcendentals=0),
        name="modulate",
    )(near(white), cosine, sine)


def walk_at(seat, chips):
    return jnp.where(seat < chips // 2, 2 * seat, 2 * (chips - 1 - seat) + 1)


def seat_of(chip, chips):
    return jnp.where(chip % 2 == 0, chip // 2, chips - 1 - chip // 2)


def correlate(modulated, groups, chips, shape, onto=None):
    flat = [piece for _, mine, other in groups for piece in (*mine, *other)]
    members = shape[1]
    extra = [] if onto is None else [onto]
    count = len(groups)

    def body(modulated, *rest):
        pieces = rest[: len(flat)]
        out, block, tile, sems = rest[len(flat) + len(extra) :]
        place = lax.axis_index("blk")
        core = lax.rem(place, 2)
        seat = seat_of(lax.div(place, 2), chips)
        at = 0
        for g, (_, mine, other) in enumerate(groups):
            for side, parts in ((core, mine), (1 - core, other)):
                rows = pl.ds(pl.multiple_of((2 * g + side) * members, members), members)
                left = 0
                for part in parts:
                    block[rows, left : left + part.shape[1]] = pieces[at][...]
                    left += part.shape[1]
                    at += 1
        copies = []
        lags = shape[0] // PARTS
        for part in range(PARTS):
            sums = lax.dot_general(
                modulated[part * lags * members : (part + 1) * lags * members, :],
                block[...],
                (((1,), (1,)), ((), ())),
                preferred_element_type=jnp.float32,
            ).reshape(lags, members, 2 * count * members)
            some = pl.ds(part * lags, lags)
            for g, (ahead, _, _) in enumerate(groups):
                tile[g, some] = sums[:, :, 2 * g * members : 2 * (g + 1) * members]
                home = walk_at(lax.rem(seat + ahead + chips, chips), chips)
                columns = pl.ds(pl.multiple_of(home * (2 * members), 2 * members), 2 * members)
                copy = pltpu.make_async_copy(
                    tile.at[g, some], out.at[some, :, columns], sems.at[g, part]
                )
                copy.start()
                copies.append(copy)
        for copy in copies:
            copy.wait()

    vmem = pl.BlockSpec(memory_space=pltpu.VMEM)
    anywhere = pl.BlockSpec(memory_space=pl.ANY)
    return pl.pallas_call(
        body,
        out_shape=jax.ShapeDtypeStruct(shape, jnp.float32),
        in_specs=[vmem] * (1 + len(flat)) + [anywhere] * len(extra),
        out_specs=anywhere,
        scratch_shapes=[
            pltpu.VMEM((count * 2 * members, modulated.shape[1]), jnp.bfloat16),
            pltpu.VMEM((count, shape[0], members, 2 * members), jnp.float32),
            pltpu.SemaphoreType.DMA((count, PARTS)),
        ],
        input_output_aliases={} if onto is None else {1 + len(flat): 0},
        compiler_params=pltpu.CompilerParams(vmem_limit_bytes=ROOM),
        cost_estimate=pl.CostEstimate(
            flops=4 * count * members * modulated.size, bytes_accessed=0, transcendentals=0
        ),
        name="correlate",
    )(near(modulated), *[near(piece) for piece in flat], *extra)


def per_device(spectra, gap_mask):
    devices = lax.axis_size("blk")
    chips = devices // 2
    walk = list(range(0, chips, 2)) + list(range(1, chips, 2))[::-1]
    members = spectra.shape[1]
    shape = (LAGS, members, devices * members)

    def shift(array, by):
        pairs = [
            (2 * walk[i] + c, 2 * walk[(i + by) % chips] + c) for i in range(chips) for c in range(2)
        ]
        return lax.ppermute(array, "blk", pairs)

    def swap(array):
        return lax.ppermute(array, "blk", [(i, i ^ 1) for i in range(devices)])

    def add(groups, out):
        return correlate(modulated, groups, chips, shape, onto=out)

    white = whiten(spectra, gap_mask)
    modulated = modulate(white, gap_mask.shape[1])
    half = white.shape[1] // 2

    up, down = white, white
    out = add([(0, (white,), (swap(white),))], None)
    final = chips // 2
    for step in range(1, final):
        up = shift(up, 1)
        down = shift(down, -1)
        groups = [(-step, (up,), (swap(up),)), (step, (down,), (swap(down),))]
        out = add(groups, out)
    up = shift(up[:, :half], 1)
    down = shift(down[:, half:], -1)
    last = (final, (up, down), (swap(up), swap(down)))
    return add([last], out)


def solution(mesh):
    placed = (P(None, ("group", "blk"), None), P(("group", "blk"), None))
    return jax.shard_map(
        per_device,
        mesh=mesh,
        in_specs=placed,
        out_specs=P(None, ("group", "blk"), None),
        check_vma=False,
    )
```

profile of v0, /device:TPU:0, one launch (start us, length us, event | category | flops | bytes accessed | tf_op | source)
XLA Modules:
  0.0 34.8 jit_solution(8593035837157927746)
XLA Ops:
  0.0 1.3 %whiten.1.white.rest_0_ = bf16[64,1536]{1,0:T(8,128)(2,1)S(1)} custom-call(bf16[2,64,768]{2,1,0:T(8,128)(2,1)} %spectra.1, s32[48,64]{1,0:T(8,128)} %bitcast.1), custom_call_target="tpu_custom_call" | custom-call | tf_op jit(solution)/shard_map/whiten/pallas_call | solution.py:69
  1.3 3.1 %collective-permute-start = (bf16[64,1536]{1,0:T(8,128)(2,1)S(1)}, bf16[64,1536]{1,0:T(8,128)(2,1)S(1)}, u32[]{:S(2)}, u32[]{:S(2)}) collective-permute-start(bf16[64,1536]{1,0:T(8,128)(2,1)S(1)} %whiten.1.white.rest_0_), channel_id=1, source_target_pairs={{0,4},{1,5},{4,8},{5,9},{8,12},{9,13},{12,14},{13,15},{14,10},{15,... | collective-permute-start | bytes 589832 | tf_op jit(solution)/shard_map/ppermute | solution.py:185
  4.4 4.8 %collective-permute-done.rest_0_ = bf16[64,1536]{1,0:T(8,128)(2,1)S(1)} collective-permute-done((bf16[64,1536]{1,0:T(8,128)(2,1)S(1)}, bf16[64,1536]{1,0:T(8,128)(2,1)S(1)}, u32[]{:S(2)}, u32[]{:S(2)}) %collective-permute-start) | collective-permute-done | bytes 196640 | tf_op jit(solution)/shard_map/ppermute | solution.py:185
  9.2 1.8 %collective-permute-start.1 = (bf16[64,1536]{1,0:T(8,128)(2,1)S(1)}, bf16[64,1536]{1,0:T(8,128)(2,1)S(1)}, u32[]{:S(2)}, u32[]{:S(2)}) collective-permute-start(bf16[64,1536]{1,0:T(8,128)(2,1)S(1)} %collective-permute-done.rest_0_), channel_id=1, source_target_pairs={{0,4},{1,5},{4,8},{5,9},{8,12},{9,13},{12,14},{13,15},{14,10},{15,... | collective-permute-start | bytes 589832 | tf_op jit(solution)/shard_map/ppermute | solution.py:185
  11.0 0.2 collective-permute-start.5
  11.3 0.5 %collective-permute-start.14 = (bf16[64,1536]{1,0:T(8,128)(2,1)S(1)}, bf16[64,1536]{1,0:T(8,128)(2,1)S(1)}, u32[]{:S(2)}, u32[]{:S(2)}) collective-permute-start(bf16[64,1536]{1,0:T(8,128)(2,1)S(1)} %collective-permute-done.rest_0_), channel_id=1, source_target_pairs={{0,1},{1,0},{2,3},{3,2},{4,5},{5,4},{6,7},{7,6},{8,9},{9,8},{10,11... | collective-permute-start | bytes 589832 | tf_op jit(solution)/shard_map/ppermute | solution.py:188
  11.8 3.5 %collective-permute-done.1.rest_0_ = bf16[64,1536]{1,0:T(8,128)(2,1)S(1)} collective-permute-done((bf16[64,1536]{1,0:T(8,128)(2,1)S(1)}, bf16[64,1536]{1,0:T(8,128)(2,1)S(1)}, u32[]{:S(2)}, u32[]{:S(2)}) %collective-permute-start.1) | collective-permute-done | bytes 196640 | tf_op jit(solution)/shard_map/ppermute | solution.py:185
  15.3 1.5 %collective-permute-start.2 = (bf16[64,1536]{1,0:T(8,128)(2,1)S(1)}, bf16[64,1536]{1,0:T(8,128)(2,1)S(1)}, u32[]{:S(2)}, u32[]{:S(2)}) collective-permute-start(bf16[64,1536]{1,0:T(8,128)(2,1)S(1)} %collective-permute-done.1.rest_0_), channel_id=1, source_target_pairs={{0,4},{1,5},{4,8},{5,9},{8,12},{9,13},{12,14},{13,15},{14,10},{15,... | collective-permute-start | bytes 589832 | tf_op jit(solution)/shard_map/ppermute | solution.py:185
  16.8 0.5 %collective-permute-start.6 = (bf16[64,1536]{1,0:T(8,128)(2,1)S(1)}, bf16[64,1536]{1,0:T(8,128)(2,1)S(1)}, u32[]{:S(2)}, u32[]{:S(2)}) collective-permute-start(bf16[64,1536]{1,0:T(8,128)(2,1)S(1)} %collective-permute-done.5.rest_2_), channel_id=1, source_target_pairs={{0,2},{1,3},{4,0},{5,1},{8,4},{9,5},{12,8},{13,9},{14,12},{15,13},... | collective-permute-start | bytes 589832 | tf_op jit(solution)/shard_map/ppermute | solution.py:185
  17.3 0.5 %collective-permute-start.12 = (bf16[64,1536]{1,0:T(8,128)(2,1)S(1)}, bf16[64,1536]{1,0:T(8,128)(2,1)S(1)}, u32[]{:S(2)}, u32[]{:S(2)}) collective-permute-start(bf16[64,1536]{1,0:T(8,128)(2,1)S(1)} %collective-permute-done.1.rest_0_), channel_id=1, source_target_pairs={{0,1},{1,0},{2,3},{3,2},{4,5},{5,4},{6,7},{7,6},{8,9},{9,8},{10,11... | collective-permute-start | bytes 589832 | tf_op jit(solution)/shard_map/ppermute | solution.py:188
  17.9 3.1 %collective-permute-done.2.rest_0_ = bf16[64,1536]{1,0:T(8,128)(2,1)S(1)} collective-permute-done((bf16[64,1536]{1,0:T(8,128)(2,1)S(1)}, bf16[64,1536]{1,0:T(8,128)(2,1)S(1)}, u32[]{:S(2)}, u32[]{:S(2)}) %collective-permute-start.2) | collective-permute-done | bytes 196640 | tf_op jit(solution)/shard_map/ppermute | solution.py:185
  21.0 1.5 %collective-permute-done.6.rest_2_ = bf16[64,1536]{1,0:T(8,128)(2,1)S(1)} collective-permute-done((bf16[64,1536]{1,0:T(8,128)(2,1)S(1)}, bf16[64,1536]{1,0:T(8,128)(2,1)S(1)}, u32[]{:S(2)}, u32[]{:S(2)}) %collective-permute-start.6) | collective-permute-done | bytes 196640 | tf_op jit(solution)/shard_map/ppermute | solution.py:185
  22.5 1.6 %collective-permute-start.3 = (bf16[64,768]{1,0:T(8,128)(2,1)S(1)}, bf16[64,768]{1,0:T(8,128)(2,1)S(1)}, u32[]{:S(2)}, u32[]{:S(2)}) collective-permute-start(bf16[64,768]{1,0:T(8,128)(2,1)S(1)} %slice.8), channel_id=1, source_target_pairs={{0,4},{1,5},{4,8},{5,9},{8,12},{9,13},{12,14},{13,15},{14,10},{15,... | collective-permute-start | bytes 294920 | tf_op jit(solution)/shard_map/ppermute | solution.py:185
  24.2 0.5 %collective-permute-start.7 = (bf16[64,768]{1,0:T(8,128)(2,1)S(1)}, bf16[64,768]{1,0:T(8,128)(2,1)S(1)}, u32[]{:S(2)}, u32[]{:S(2)}) collective-permute-start(bf16[64,768]{1,0:T(8,128)(2,1)S(1)} %slice.9), channel_id=1, source_target_pairs={{0,2},{1,3},{4,0},{5,1},{8,4},{9,5},{12,8},{13,9},{14,12},{15,13},... | collective-permute-start | bytes 294920 | tf_op jit(solution)/shard_map/ppermute | solution.py:185
  24.6 0.7 %copy-done = f32[8,1,768]{2,1,0:T(1,128)S(1)} copy-done((f32[8,1,768]{2,1,0:T(1,128)S(1)}, f32[8,1,768]{2,1,0:T(1,128)}, u32[]{:S(2)}) %copy-start) | copy-done | bytes 24600
  25.4 0.7 %copy-done.1 = f32[8,1,768]{2,1,0:T(1,128)S(1)} copy-done((f32[8,1,768]{2,1,0:T(1,128)S(1)}, f32[8,1,768]{2,1,0:T(1,128)}, u32[]{:S(2)}) %copy-start.1) | copy-done | bytes 24600
  26.1 0.4 %modulate.1.modulated = bf16[512,1536]{1,0:T(8,128)(2,1)S(1)} custom-call(bf16[64,1536]{1,0:T(8,128)(2,1)S(1)} %whiten.1.white.rest_0_, f32[8,1,768]{2,1,0:T(1,128)S(1)} %copy-done, f32[8,1,768]{2,1,0:T(1,128)S(1)} %copy-done.1), custom_call_target="tpu_custom_call" | custom-call | flops 9437184 | tf_op jit(solution)/shard_map/modulate/pallas_call | solution.py:93
  26.5 1.3 %correlate.5.rest_4_ = f32[8,64,1024]{2,1,0:T(8,128)} custom-call(bf16[512,1536]{1,0:T(8,128)(2,1)S(1)} %modulate.1.modulated, bf16[64,1536]{1,0:T(8,128)(2,1)S(1)} %whiten.1.white.rest_0_, bf16[64,1536]{1,0:T(8,128)(2,1)S(1)} %collective-permute-done.16.rest_1_), custom_call_target="tpu_custom_call" | custom-call | flops 201326592 | tf_op jit(solution)/shard_map/correlate/pallas_call | solution.py:155
  27.8 0.1 collective-permute-start.8
  27.9 1.2 %collective-permute-done.7.rest_1_ = bf16[64,768]{1,0:T(8,128)(2,1)S(1)} collective-permute-done((bf16[64,768]{1,0:T(8,128)(2,1)S(1)}, bf16[64,768]{1,0:T(8,128)(2,1)S(1)}, u32[]{:S(2)}, u32[]{:S(2)}) %collective-permute-start.7) | collective-permute-done | bytes 98336 | tf_op jit(solution)/shard_map/ppermute | solution.py:185
  29.1 1.5 %correlate.6.rest_4_ = f32[8,64,1024]{2,1,0:T(8,128)} custom-call(bf16[512,1536]{1,0:T(8,128)(2,1)S(1)} %modulate.1.modulated, bf16[64,1536]{1,0:T(8,128)(2,1)S(1)} %collective-permute-done.rest_0_, bf16[64,1536]{1,0:T(8,128)(2,1)S(1)} %collective-permute-done.14.rest_1_, ...), custom_call_target="tpu_custom_call", output_to_operand_aliasing={{}: (5, {})} | custom-call | flops 402653184 | tf_op jit(solution)/shard_map/correlate/pallas_call | solution.py:155
  30.6 1.4 %correlate.7.rest_4_ = f32[8,64,1024]{2,1,0:T(8,128)} custom-call(bf16[512,1536]{1,0:T(8,128)(2,1)S(1)} %modulate.1.modulated, bf16[64,1536]{1,0:T(8,128)(2,1)S(1)} %collective-permute-done.1.rest_0_, bf16[64,1536]{1,0:T(8,128)(2,1)S(1)} %collective-permute-done.12.rest_1_, ...), custom_call_target="tpu_custom_call", output_to_operand_aliasing={{}: (5, {})} | custom-call | flops 402653184 | tf_op jit(solution)/shard_map/correlate/pallas_call | solution.py:155
  32.0 1.5 %correlate.8.rest_4_ = f32[8,64,1024]{2,1,0:T(8,128)} custom-call(bf16[512,1536]{1,0:T(8,128)(2,1)S(1)} %modulate.1.modulated, bf16[64,1536]{1,0:T(8,128)(2,1)S(1)} %collective-permute-done.2.rest_0_, bf16[64,1536]{1,0:T(8,128)(2,1)S(1)} %collective-permute-done.10.rest_1_, ...), custom_call_target="tpu_custom_call", output_to_operand_aliasing={{}: (5, {})} | custom-call | flops 402653184 | tf_op jit(solution)/shard_map/correlate/pallas_call | solution.py:155
  33.5 1.3 %correlate.9 = f32[8,64,1024]{2,1,0:T(8,128)} custom-call(bf16[512,1536]{1,0:T(8,128)(2,1)S(1)} %modulate.1.modulated, bf16[64,768]{1,0:T(8,128)(2,1)S(1)} %collective-permute-done.3.rest_0_, bf16[64,768]{1,0:T(8,128)(2,1)S(1)} %collective-permute-done.7.rest_1_, bf16[64,768]{1,0:T(8,128)(2,1)S(1)} %collective-permute-done.8.rest_2_, ...), custom_call_target="tpu_custom_call", output_to_operand_aliasing={{}: (5, {})} | custom-call | flops 201326592 | tf_op jit(solution)/shard_map/correlate/pallas_call | solution.py:155
  (23 shorter events, 0.1 us)
Async XLA Ops:
  1.3 7.9 %collective-permute-start = (bf16[64,1536]{1,0:T(8,128)(2,1)S(1)}, bf16[64,1536]{1,0:T(8,128)(2,1)S(1)}, u32[]{:S(2)}, u32[]{:S(2)}) collective-permute-start(bf16[64,1536]{1,0:T(8,128)(2,1)S(1)} %whiten.1.white.rest_0_), channel_id=1, source_target_pairs={{0,4},{1,5},{4,8},{5,9},{8,12},{9,13},{12,14},{13,15},{14,10},{15,... | collective-permute-start | bytes 589832 | tf_op jit(solution)/shard_map/ppermute | solution.py:185
  4.4 6.6 %collective-permute-start.4 = (bf16[64,1536]{1,0:T(8,128)(2,1)S(1)}, bf16[64,1536]{1,0:T(8,128)(2,1)S(1)}, u32[]{:S(2)}, u32[]{:S(2)}) collective-permute-start(bf16[64,1536]{1,0:T(8,128)(2,1)S(1)} %whiten.1.white.rest_0_), channel_id=1, source_target_pairs={{0,2},{1,3},{4,0},{5,1},{8,4},{9,5},{12,8},{13,9},{14,12},{15,13},... | collective-permute-start | bytes 589832 | tf_op jit(solution)/shard_map/ppermute | solution.py:185
  9.2 6.1 %collective-permute-start.1 = (bf16[64,1536]{1,0:T(8,128)(2,1)S(1)}, bf16[64,1536]{1,0:T(8,128)(2,1)S(1)}, u32[]{:S(2)}, u32[]{:S(2)}) collective-permute-start(bf16[64,1536]{1,0:T(8,128)(2,1)S(1)} %collective-permute-done.rest_0_), channel_id=1, source_target_pairs={{0,4},{1,5},{4,8},{5,9},{8,12},{9,13},{12,14},{13,15},{14,10},{15,... | collective-permute-start | bytes 589832 | tf_op jit(solution)/shard_map/ppermute | solution.py:185
  11.0 5.8 %collective-permute-start.5 = (bf16[64,1536]{1,0:T(8,128)(2,1)S(1)}, bf16[64,1536]{1,0:T(8,128)(2,1)S(1)}, u32[]{:S(2)}, u32[]{:S(2)}) collective-permute-start(bf16[64,1536]{1,0:T(8,128)(2,1)S(1)} %collective-permute-done.4.rest_2_), channel_id=1, source_target_pairs={{0,2},{1,3},{4,0},{5,1},{8,4},{9,5},{12,8},{13,9},{14,12},{15,13},... | collective-permute-start | bytes 589832 | tf_op jit(solution)/shard_map/ppermute | solution.py:185
  11.3 6.1 %collective-permute-start.16 = (bf16[64,1536]{1,0:T(8,128)(2,1)S(1)}, bf16[64,1536]{1,0:T(8,128)(2,1)S(1)}, u32[]{:S(2)}, u32[]{:S(2)}) collective-permute-start(bf16[64,1536]{1,0:T(8,128)(2,1)S(1)} %whiten.1.white.rest_0_), channel_id=1, source_target_pairs={{0,1},{1,0},{2,3},{3,2},{4,5},{5,4},{6,7},{7,6},{8,9},{9,8},{10,11... | collective-permute-start | bytes 589832 | tf_op jit(solution)/shard_map/ppermute | solution.py:188
  11.3 6.6 %collective-permute-start.14 = (bf16[64,1536]{1,0:T(8,128)(2,1)S(1)}, bf16[64,1536]{1,0:T(8,128)(2,1)S(1)}, u32[]{:S(2)}, u32[]{:S(2)}) collective-permute-start(bf16[64,1536]{1,0:T(8,128)(2,1)S(1)} %collective-permute-done.rest_0_), channel_id=1, source_target_pairs={{0,1},{1,0},{2,3},{3,2},{4,5},{5,4},{6,7},{7,6},{8,9},{9,8},{10,11... | collective-permute-start | bytes 589832 | tf_op jit(solution)/shard_map/ppermute | solution.py:188
  15.3 5.7 %collective-permute-start.2 = (bf16[64,1536]{1,0:T(8,128)(2,1)S(1)}, bf16[64,1536]{1,0:T(8,128)(2,1)S(1)}, u32[]{:S(2)}, u32[]{:S(2)}) collective-permute-start(bf16[64,1536]{1,0:T(8,128)(2,1)S(1)} %collective-permute-done.1.rest_0_), channel_id=1, source_target_pairs={{0,4},{1,5},{4,8},{5,9},{8,12},{9,13},{12,14},{13,15},{14,10},{15,... | collective-permute-start | bytes 589832 | tf_op jit(solution)/shard_map/ppermute | solution.py:185
  16.8 5.7 %collective-permute-start.6 = (bf16[64,1536]{1,0:T(8,128)(2,1)S(1)}, bf16[64,1536]{1,0:T(8,128)(2,1)S(1)}, u32[]{:S(2)}, u32[]{:S(2)}) collective-permute-start(bf16[64,1536]{1,0:T(8,128)(2,1)S(1)} %collective-permute-done.5.rest_2_), channel_id=1, source_target_pairs={{0,2},{1,3},{4,0},{5,1},{8,4},{9,5},{12,8},{13,9},{14,12},{15,13},... | collective-permute-start | bytes 589832 | tf_op jit(solution)/shard_map/ppermute | solution.py:185
  17.3 5.2 %collective-permute-start.15 = (bf16[64,1536]{1,0:T(8,128)(2,1)S(1)}, bf16[64,1536]{1,0:T(8,128)(2,1)S(1)}, u32[]{:S(2)}, u32[]{:S(2)}) collective-permute-start(bf16[64,1536]{1,0:T(8,128)(2,1)S(1)} %collective-permute-done.4.rest_2_), channel_id=1, source_target_pairs={{0,1},{1,0},{2,3},{3,2},{4,5},{5,4},{6,7},{7,6},{8,9},{9,8},{10,11... | collective-permute-start | bytes 589832 | tf_op jit(solution)/shard_map/ppermute | solution.py:188
  17.3 6.8 %collective-permute-start.12 = (bf16[64,1536]{1,0:T(8,128)(2,1)S(1)}, bf16[64,1536]{1,0:T(8,128)(2,1)S(1)}, u32[]{:S(2)}, u32[]{:S(2)}) collective-permute-start(bf16[64,1536]{1,0:T(8,128)(2,1)S(1)} %collective-permute-done.1.rest_0_), channel_id=1, source_target_pairs={{0,1},{1,0},{2,3},{3,2},{4,5},{5,4},{6,7},{7,6},{8,9},{9,8},{10,11... | collective-permute-start | bytes 589832 | tf_op jit(solution)/shard_map/ppermute | solution.py:188
  17.8 12.7 %collective-permute-start.13 = (bf16[64,1536]{1,0:T(8,128)(2,1)S(1)}, bf16[64,1536]{1,0:T(8,128)(2,1)S(1)}, u32[]{:S(2)}, u32[]{:S(2)}) collective-permute-start(bf16[64,1536]{1,0:T(8,128)(2,1)S(1)} %collective-permute-done.5.rest_2_), channel_id=1, source_target_pairs={{0,1},{1,0},{2,3},{3,2},{4,5},{5,4},{6,7},{7,6},{8,9},{9,8},{10,11... | collective-permute-start | bytes 589832 | tf_op jit(solution)/shard_map/ppermute | solution.py:188
  21.0 11.0 %collective-permute-start.10 = (bf16[64,1536]{1,0:T(8,128)(2,1)S(1)}, bf16[64,1536]{1,0:T(8,128)(2,1)S(1)}, u32[]{:S(2)}, u32[]{:S(2)}) collective-permute-start(bf16[64,1536]{1,0:T(8,128)(2,1)S(1)} %collective-permute-done.2.rest_0_), channel_id=1, source_target_pairs={{0,1},{1,0},{2,3},{3,2},{4,5},{5,4},{6,7},{7,6},{8,9},{9,8},{10,11... | collective-permute-start | bytes 589832 | tf_op jit(solution)/shard_map/ppermute | solution.py:188
  22.5 9.5 %collective-permute-start.11 = (bf16[64,1536]{1,0:T(8,128)(2,1)S(1)}, bf16[64,1536]{1,0:T(8,128)(2,1)S(1)}, u32[]{:S(2)}, u32[]{:S(2)}) collective-permute-start(bf16[64,1536]{1,0:T(8,128)(2,1)S(1)} %collective-permute-done.6.rest_2_), channel_id=1, source_target_pairs={{0,1},{1,0},{2,3},{3,2},{4,5},{5,4},{6,7},{7,6},{8,9},{9,8},{10,11... | collective-permute-start | bytes 589832 | tf_op jit(solution)/shard_map/ppermute | solution.py:188
  22.5 5.3 %collective-permute-start.3 = (bf16[64,768]{1,0:T(8,128)(2,1)S(1)}, bf16[64,768]{1,0:T(8,128)(2,1)S(1)}, u32[]{:S(2)}, u32[]{:S(2)}) collective-permute-start(bf16[64,768]{1,0:T(8,128)(2,1)S(1)} %slice.8), channel_id=1, source_target_pairs={{0,4},{1,5},{4,8},{5,9},{8,12},{9,13},{12,14},{13,15},{14,10},{15,... | collective-permute-start | bytes 294920 | tf_op jit(solution)/shard_map/ppermute | solution.py:185
  24.2 4.9 %collective-permute-start.7 = (bf16[64,768]{1,0:T(8,128)(2,1)S(1)}, bf16[64,768]{1,0:T(8,128)(2,1)S(1)}, u32[]{:S(2)}, u32[]{:S(2)}) collective-permute-start(bf16[64,768]{1,0:T(8,128)(2,1)S(1)} %slice.9), channel_id=1, source_target_pairs={{0,2},{1,3},{4,0},{5,1},{8,4},{9,5},{12,8},{13,9},{14,12},{15,13},... | collective-permute-start | bytes 294920 | tf_op jit(solution)/shard_map/ppermute | solution.py:185
  24.6 0.7 %copy-start = (f32[8,1,768]{2,1,0:T(1,128)S(1)}, f32[8,1,768]{2,1,0:T(1,128)}, u32[]{:S(2)}) copy-start(f32[8,1,768]{2,1,0:T(1,128)} %constant.4.clone.cosine) | copy-start | bytes 73732
  25.4 0.7 %copy-start.1 = (f32[8,1,768]{2,1,0:T(1,128)S(1)}, f32[8,1,768]{2,1,0:T(1,128)}, u32[]{:S(2)}) copy-start(f32[8,1,768]{2,1,0:T(1,128)} %constant.5.clone.sine) | copy-start | bytes 73732
  27.8 5.7 %collective-permute-start.8 = (bf16[64,768]{1,0:T(8,128)(2,1)S(1)}, bf16[64,768]{1,0:T(8,128)(2,1)S(1)}, u32[]{:S(2)}, u32[]{:S(2)}) collective-permute-start(bf16[64,768]{1,0:T(8,128)(2,1)S(1)} %collective-permute-done.3.rest_0_), channel_id=1, source_target_pairs={{0,1},{1,0},{2,3},{3,2},{4,5},{5,4},{6,7},{7,6},{8,9},{9,8},{10,11... | collective-permute-start | bytes 294920 | tf_op jit(solution)/shard_map/ppermute | solution.py:188
  29.1 4.4 %collective-permute-start.9 = (bf16[64,768]{1,0:T(8,128)(2,1)S(1)}, bf16[64,768]{1,0:T(8,128)(2,1)S(1)}, u32[]{:S(2)}, u32[]{:S(2)}) collective-permute-start(bf16[64,768]{1,0:T(8,128)(2,1)S(1)} %collective-permute-done.7.rest_1_), channel_id=1, source_target_pairs={{0,1},{1,0},{2,3},{3,2},{4,5},{5,4},{6,7},{7,6},{8,9},{9,8},{10,11... | collective-permute-start | bytes 294920 | tf_op jit(solution)/shard_map/ppermute | solution.py:188
where the time goes:
time: 35.1 us; the launch traced here: 34.8 us
  waiting for transfers between devices  14.2 us (40%)
  starting transfers between devices  10.4 us (30%)
  Pallas kernels  8.61 us (25%)
  local copies, waits for them, and re-layouts  1.49 us (4%)
    ppermute x8, waiting for transfers between devices, shift(): return lax.ppermute(array, 'blk', pairs)  14.1 us
    ppermute x8, starting transfers between devices, shift(): return lax.ppermute(array, 'blk', pairs)  9.24 us
    pallas_call x5, Pallas kernels, correlate(): pl.pallas_call(body, out_shape=jax.ShapeDtypeStruct(shape, jnp.float32),...  6.95 us
    unnamed x4, local copies, waits for them, and re-layouts  1.47 us
    pallas_call x1, Pallas kernels, whiten(): pl.pallas_call(whiten_body, out_shape=pltpu.VMEM((members, 2 * wide), jnp...  1.27 us
    ppermute x9, starting transfers between devices, swap(): return lax.ppermute(array, 'blk', [(i, i ^ 1) for i in range(devices)])  1.17 us
  transfers between devices with their start and end apart: 17, of which 5 were waited for; matrix products, arithmetic and copies ran while one was open for 0% of the time, Pallas kernels for 17%

commit v1 on v0

--- a/solution.py
+++ b/solution.py
@@ -108,7 +108,7 @@
 
 
 def correlate(modulated, groups, chips, shape, onto=None):
-    flat = [piece for _, mine, other in groups for piece in (*mine, *other)]
+    flat = [piece for _, mine, other in groups for piece in (mine, other)]
     members = shape[1]
     extra = [] if onto is None else [onto]
     count = len(groups)
@@ -119,15 +119,10 @@
         place = lax.axis_index("blk")
         core = lax.rem(place, 2)
         seat = seat_of(lax.div(place, 2), chips)
-        at = 0
-        for g, (_, mine, other) in enumerate(groups):
-            for side, parts in ((core, mine), (1 - core, other)):
+        for g in range(count):
+            for side, piece in ((core, pieces[2 * g]), (1 - core, pieces[2 * g + 1])):
                 rows = pl.ds(pl.multiple_of((2 * g + side) * members, members), members)
-                left = 0
-                for part in parts:
-                    block[rows, left : left + part.shape[1]] = pieces[at][...]
-                    left += part.shape[1]
-                    at += 1
+                block[rows, :] = piece[...]
         copies = []
         lags = shape[0] // PARTS
         for part in range(PARTS):
@@ -138,9 +133,9 @@
                 preferred_element_type=jnp.float32,
             ).reshape(lags, members, 2 * count * members)
             some = pl.ds(part * lags, lags)
-            for g, (ahead, _, _) in enumerate(groups):
+            for g, (back, _, _) in enumerate(groups):
                 tile[g, some] = sums[:, :, 2 * g * members : 2 * (g + 1) * members]
-                home = walk_at(lax.rem(seat + ahead + chips, chips), chips)
+                home = walk_at(lax.rem(seat + chips - back * (1 - 2 * core), chips), chips)
                 columns = pl.ds(pl.multiple_of(home * (2 * members), 2 * members), 2 * members)
                 copy = pltpu.make_async_copy(
                     tile.at[g, some], out.at[some, :, columns], sems.at[g, part]
@@ -178,9 +173,9 @@
     members = spectra.shape[1]
     shape = (LAGS, members, devices * members)
 
-    def shift(array, by):
+    def onward(array):
         pairs = [
-            (2 * walk[i] + c, 2 * walk[(i + by) % chips] + c) for i in range(chips) for c in range(2)
+            (2 * walk[i] + c, 2 * walk[(i + 1 - 2 * c) % chips] + c) for i in range(chips) for c in range(2)
         ]
         return lax.ppermute(array, "blk", pairs)
 
@@ -192,20 +187,19 @@
 
     white = whiten(spectra, gap_mask)
     modulated = modulate(white, gap_mask.shape[1])
-    half = white.shape[1] // 2
-
-    up, down = white, white
-    out = add([(0, (white,), (swap(white),))], None)
+
+    mine, other = white, swap(white)
+    out = add([(0, mine, other)], None)
     final = chips // 2
+    waiting = []
     for step in range(1, final):
-        up = shift(up, 1)
-        down = shift(down, -1)
-        groups = [(-step, (up,), (swap(up),)), (step, (down,), (swap(down),))]
-        out = add(groups, out)
-    up = shift(up[:, :half], 1)
-    down = shift(down[:, half:], -1)
-    last = (final, (up, down), (swap(up), swap(down)))
-    return add([last], out)
+        mine = onward(mine)
+        other = onward(other)
+        out = add([(step, mine, other)] + waiting, out)
+        waiting = [(-step, swap(other), swap(mine))]
+    mine = onward(mine)
+    out = add(waiting, out)
+    return add([(final, mine, swap(mine))], out)
 
 
 def solution(mesh):

time: 35.1 us -> 35.4 us (level)
  waiting for transfers between devices: 14.2 us -> 7.6 us
  starting transfers between devices: 10.4 us -> 16.2 us
  Pallas kernels: 8.61 us -> 9.77 us
    ppermute x8 -> x7, waiting for transfers between devices: 14.1 us -> 7.57 us  [onward(): return lax.ppermute(array, 'blk', pairs)]
    ppermute x8 -> x7, starting transfers between devices: 9.24 us -> 14.1 us  [onward(): return lax.ppermute(array, 'blk', pairs)]
    pallas_call x5 -> x6, Pallas kernels: 6.95 us -> 8.11 us  [correlate(): pl.pallas_call(body, out_shape=jax.ShapeDtypeStruct(shape, jnp.float32),...]
    ppermute x9 -> x8, starting transfers between devices: 1.17 us -> 2.09 us  [swap(): return lax.ppermute(array, 'blk', [(i, i ^ 1) for i in range(devices)])]
  transfers between devices with their start and end apart: 17 -> 15, of which waited for: 5 -> 4; matrix products, arithmetic and copies ran while one was open for 0% -> 0% of each run, Pallas kernels for 17% -> 20%
where the time goes in v1:
time: 35.4 us; the launch traced here: 35.1 us
  starting transfers between devices  16.2 us (46%)
  Pallas kernels  9.77 us (28%)
  waiting for transfers between devices  7.6 us (21%)
  local copies, waits for them, and re-layouts  1.47 us (4%)
    ppermute x7, starting transfers between devices, onward(): return lax.ppermute(array, 'blk', pairs)  14.1 us
    pallas_call x6, Pallas kernels, correlate(): pl.pallas_call(body, out_shape=jax.ShapeDtypeStruct(shape, jnp.float32),...  8.11 us
    ppermute x7, waiting for transfers between devices, onward(): return lax.ppermute(array, 'blk', pairs)  7.57 us
    ppermute x8, starting transfers between devices, swap(): return lax.ppermute(array, 'blk', [(i, i ^ 1) for i in range(devices)])  2.09 us
    unnamed x4, local copies, waits for them, and re-layouts  1.47 us
    pallas_call x1, Pallas kernels, whiten(): pl.pallas_call(whiten_body, out_shape=pltpu.VMEM((members, 2 * wide), jnp...  1.27 us
  transfers between devices with their start and end apart: 15, of which 4 were waited for; matrix products, arithmetic and copies ran while one was open for 0% of the time, Pallas kernels for 20%

profile of v1, /device:TPU:0, one launch (start us, length us, event | category | flops | bytes accessed | tf_op | source)
XLA Modules:
  0.0 35.1 jit_solution(3756957080763957253)
XLA Ops:
  0.0 1.3 %whiten.1.white.rest_0_ = bf16[64,1536]{1,0:T(8,128)(2,1)S(1)} custom-call(bf16[2,64,768]{2,1,0:T(8,128)(2,1)} %spectra.1, s32[48,64]{1,0:T(8,128)} %bitcast.1), custom_call_target="tpu_custom_call" | custom-call | tf_op jit(solution)/shard_map/whiten/pallas_call | solution.py:69
  1.3 0.6 %collective-permute-start.5 = (bf16[64,1536]{1,0:T(8,128)(2,1)S(1)}, bf16[64,1536]{1,0:T(8,128)(2,1)S(1)}, u32[]{:S(2)}, u32[]{:S(2)}) collective-permute-start(bf16[64,1536]{1,0:T(8,128)(2,1)S(1)} %whiten.1.white.rest_0_), channel_id=1, source_target_pairs={{0,1},{1,0},{2,3},{3,2},{4,5},{5,4},{6,7},{7,6},{8,9},{9,8},{10,11... | collective-permute-start | bytes 589832 | tf_op jit(solution)/shard_map/ppermute | solution.py:183
  1.8 2.6 %collective-permute-start = (bf16[64,1536]{1,0:T(8,128)(2,1)S(1)}, bf16[64,1536]{1,0:T(8,128)(2,1)S(1)}, u32[]{:S(2)}, u32[]{:S(2)}) collective-permute-start(bf16[64,1536]{1,0:T(8,128)(2,1)S(1)} %whiten.1.white.rest_0_), channel_id=1, source_target_pairs={{0,4},{1,3},{4,8},{5,1},{8,12},{9,5},{12,14},{13,9},{14,10},{15,13... | collective-permute-start | bytes 589832 | tf_op jit(solution)/shard_map/ppermute | solution.py:180
  4.5 1.6 %collective-permute-start.6 = (bf16[64,1536]{1,0:T(8,128)(2,1)S(1)}, bf16[64,1536]{1,0:T(8,128)(2,1)S(1)}, u32[]{:S(2)}, u32[]{:S(2)}) collective-permute-start(bf16[64,1536]{1,0:T(8,128)(2,1)S(1)} %collective-permute-done.5.rest_1_), channel_id=1, source_target_pairs={{0,4},{1,3},{4,8},{5,1},{8,12},{9,5},{12,14},{13,9},{14,10},{15,13... | collective-permute-start | bytes 589832 | tf_op jit(solution)/shard_map/ppermute | solution.py:180
  6.0 2.0 %collective-permute-done.rest_0_ = bf16[64,1536]{1,0:T(8,128)(2,1)S(1)} collective-permute-done((bf16[64,1536]{1,0:T(8,128)(2,1)S(1)}, bf16[64,1536]{1,0:T(8,128)(2,1)S(1)}, u32[]{:S(2)}, u32[]{:S(2)}) %collective-permute-start) | collective-permute-done | bytes 196640 | tf_op jit(solution)/shard_map/ppermute | solution.py:180
  8.1 2.1 %collective-permute-start.1 = (bf16[64,1536]{1,0:T(8,128)(2,1)S(1)}, bf16[64,1536]{1,0:T(8,128)(2,1)S(1)}, u32[]{:S(2)}, u32[]{:S(2)}) collective-permute-start(bf16[64,1536]{1,0:T(8,128)(2,1)S(1)} %collective-permute-done.rest_0_), channel_id=1, source_target_pairs={{0,4},{1,3},{4,8},{5,1},{8,12},{9,5},{12,14},{13,9},{14,10},{15,13... | collective-permute-start | bytes 589832 | tf_op jit(solution)/shard_map/ppermute | solution.py:180
  10.2 2.1 %collective-permute-start.7 = (bf16[64,1536]{1,0:T(8,128)(2,1)S(1)}, bf16[64,1536]{1,0:T(8,128)(2,1)S(1)}, u32[]{:S(2)}, u32[]{:S(2)}) collective-permute-start(bf16[64,1536]{1,0:T(8,128)(2,1)S(1)} %collective-permute-done.6.rest_1_), channel_id=1, source_target_pairs={{0,4},{1,3},{4,8},{5,1},{8,12},{9,5},{12,14},{13,9},{14,10},{15,13... | collective-permute-start | bytes 589832 | tf_op jit(solution)/shard_map/ppermute | solution.py:180
  12.2 1.5 %collective-permute-done.1.rest_0_ = bf16[64,1536]{1,0:T(8,128)(2,1)S(1)} collective-permute-done((bf16[64,1536]{1,0:T(8,128)(2,1)S(1)}, bf16[64,1536]{1,0:T(8,128)(2,1)S(1)}, u32[]{:S(2)}, u32[]{:S(2)}) %collective-permute-start.1) | collective-permute-done | bytes 196640 | tf_op jit(solution)/shard_map/ppermute | solution.py:180
  13.7 2.1 %collective-permute-start.2 = (bf16[64,1536]{1,0:T(8,128)(2,1)S(1)}, bf16[64,1536]{1,0:T(8,128)(2,1)S(1)}, u32[]{:S(2)}, u32[]{:S(2)}) collective-permute-start(bf16[64,1536]{1,0:T(8,128)(2,1)S(1)} %collective-permute-done.1.rest_0_), channel_id=1, source_target_pairs={{0,4},{1,3},{4,8},{5,1},{8,12},{9,5},{12,14},{13,9},{14,10},{15,13... | collective-permute-start | bytes 589832 | tf_op jit(solution)/shard_map/ppermute | solution.py:180
  15.8 0.5 %collective-permute-start.13 = (bf16[64,1536]{1,0:T(8,128)(2,1)S(1)}, bf16[64,1536]{1,0:T(8,128)(2,1)S(1)}, u32[]{:S(2)}, u32[]{:S(2)}) collective-permute-start(bf16[64,1536]{1,0:T(8,128)(2,1)S(1)} %collective-permute-done.6.rest_1_), channel_id=1, source_target_pairs={{0,1},{1,0},{2,3},{3,2},{4,5},{5,4},{6,7},{7,6},{8,9},{9,8},{10,11... | collective-permute-start | bytes 589832 | tf_op jit(solution)/shard_map/ppermute | solution.py:183
  16.3 1.6 %collective-permute-start.8 = (bf16[64,1536]{1,0:T(8,128)(2,1)S(1)}, bf16[64,1536]{1,0:T(8,128)(2,1)S(1)}, u32[]{:S(2)}, u32[]{:S(2)}) collective-permute-start(bf16[64,1536]{1,0:T(8,128)(2,1)S(1)} %collective-permute-done.7.rest_1_), channel_id=1, source_target_pairs={{0,4},{1,3},{4,8},{5,1},{8,12},{9,5},{12,14},{13,9},{14,10},{15,13... | collective-permute-start | bytes 589832 | tf_op jit(solution)/shard_map/ppermute | solution.py:180
  17.9 1.5 %collective-permute-done.2.rest_0_ = bf16[64,1536]{1,0:T(8,128)(2,1)S(1)} collective-permute-done((bf16[64,1536]{1,0:T(8,128)(2,1)S(1)}, bf16[64,1536]{1,0:T(8,128)(2,1)S(1)}, u32[]{:S(2)}, u32[]{:S(2)}) %collective-permute-start.2) | collective-permute-done | bytes 196640 | tf_op jit(solution)/shard_map/ppermute | solution.py:180
  19.4 2.1 %collective-permute-start.3 = (bf16[64,1536]{1,0:T(8,128)(2,1)S(1)}, bf16[64,1536]{1,0:T(8,128)(2,1)S(1)}, u32[]{:S(2)}, u32[]{:S(2)}) collective-permute-start(bf16[64,1536]{1,0:T(8,128)(2,1)S(1)} %collective-permute-done.2.rest_0_), channel_id=1, source_target_pairs={{0,4},{1,3},{4,8},{5,1},{8,12},{9,5},{12,14},{13,9},{14,10},{15,13... | collective-permute-start | bytes 589832 | tf_op jit(solution)/shard_map/ppermute | solution.py:180
  21.5 0.5 %collective-permute-start.11 = (bf16[64,1536]{1,0:T(8,128)(2,1)S(1)}, bf16[64,1536]{1,0:T(8,128)(2,1)S(1)}, u32[]{:S(2)}, u32[]{:S(2)}) collective-permute-start(bf16[64,1536]{1,0:T(8,128)(2,1)S(1)} %collective-permute-done.7.rest_1_), channel_id=1, source_target_pairs={{0,1},{1,0},{2,3},{3,2},{4,5},{5,4},{6,7},{7,6},{8,9},{9,8},{10,11... | collective-permute-start | bytes 589832 | tf_op jit(solution)/shard_map/ppermute | solution.py:183
  22.1 0.4 %collective-permute-start.9 = (bf16[64,1536]{1,0:T(8,128)(2,1)S(1)}, bf16[64,1536]{1,0:T(8,128)(2,1)S(1)}, u32[]{:S(2)}, u32[]{:S(2)}) collective-permute-start(bf16[64,1536]{1,0:T(8,128)(2,1)S(1)} %collective-permute-done.8.rest_1_), channel_id=1, source_target_pairs={{0,1},{1,0},{2,3},{3,2},{4,5},{5,4},{6,7},{7,6},{8,9},{9,8},{10,11... | collective-permute-start | bytes 589832 | tf_op jit(solution)/shard_map/ppermute | solution.py:183
  22.5 2.6 %collective-permute-done.3.rest_0_ = bf16[64,1536]{1,0:T(8,128)(2,1)S(1)} collective-permute-done((bf16[64,1536]{1,0:T(8,128)(2,1)S(1)}, bf16[64,1536]{1,0:T(8,128)(2,1)S(1)}, u32[]{:S(2)}, u32[]{:S(2)}) %collective-permute-start.3) | collective-permute-done | bytes 196640 | tf_op jit(solution)/shard_map/ppermute | solution.py:180
  25.1 0.7 %copy-done = f32[8,1,768]{2,1,0:T(1,128)S(1)} copy-done((f32[8,1,768]{2,1,0:T(1,128)S(1)}, f32[8,1,768]{2,1,0:T(1,128)}, u32[]{:S(2)}) %copy-start) | copy-done | bytes 24600
  25.8 0.7 %copy-done.1 = f32[8,1,768]{2,1,0:T(1,128)S(1)} copy-done((f32[8,1,768]{2,1,0:T(1,128)S(1)}, f32[8,1,768]{2,1,0:T(1,128)}, u32[]{:S(2)}) %copy-start.1) | copy-done | bytes 24600
  26.9 1.3 %correlate.6.rest_2_ = f32[8,64,1024]{2,1,0:T(8,128)} custom-call(bf16[512,1536]{1,0:T(8,128)(2,1)S(1)} %modulate.1.modulated, bf16[64,1536]{1,0:T(8,128)(2,1)S(1)} %whiten.1.white.rest_0_, bf16[64,1536]{1,0:T(8,128)(2,1)S(1)} %collective-permute-done.5.rest_1_), custom_call_target="tpu_custom_call" | custom-call | flops 201326592 | tf_op jit(solution)/shard_map/correlate/pallas_call | solution.py:150
  28.2 1.3 %correlate.7.rest_4_ = f32[8,64,1024]{2,1,0:T(8,128)} custom-call(bf16[512,1536]{1,0:T(8,128)(2,1)S(1)} %modulate.1.modulated, bf16[64,1536]{1,0:T(8,128)(2,1)S(1)} %collective-permute-done.rest_0_, bf16[64,1536]{1,0:T(8,128)(2,1)S(1)} %collective-permute-done.6.rest_1_, f32[8,64,1024]{2,1,0:T(8,128)} %correlate.6.rest_2_), custom_call_target="tpu_custom_call", output_to_operand_aliasing={{}: (3, {})} | custom-call | flops 201326592 | tf_op jit(solution)/shard_map/correlate/pallas_call | solution.py:150
  29.6 1.4 %correlate.8.rest_4_ = f32[8,64,1024]{2,1,0:T(8,128)} custom-call(bf16[512,1536]{1,0:T(8,128)(2,1)S(1)} %modulate.1.modulated, bf16[64,1536]{1,0:T(8,128)(2,1)S(1)} %collective-permute-done.1.rest_0_, bf16[64,1536]{1,0:T(8,128)(2,1)S(1)} %collective-permute-done.7.rest_1_, ...), custom_call_target="tpu_custom_call", output_to_operand_aliasing={{}: (5, {})} | custom-call | flops 402653184 | tf_op jit(solution)/shard_map/correlate/pallas_call | solution.py:150
  31.0 1.5 %correlate.9.rest_2_ = f32[8,64,1024]{2,1,0:T(8,128)} custom-call(bf16[512,1536]{1,0:T(8,128)(2,1)S(1)} %modulate.1.modulated, bf16[64,1536]{1,0:T(8,128)(2,1)S(1)} %collective-permute-done.2.rest_0_, bf16[64,1536]{1,0:T(8,128)(2,1)S(1)} %collective-permute-done.8.rest_1_, ...), custom_call_target="tpu_custom_call", output_to_operand_aliasing={{}: (5, {})} | custom-call | flops 402653184 | tf_op jit(solution)/shard_map/correlate/pallas_call | solution.py:150
  32.5 1.3 %correlate.10.rest_2_ = f32[8,64,1024]{2,1,0:T(8,128)} custom-call(bf16[512,1536]{1,0:T(8,128)(2,1)S(1)} %modulate.1.modulated, bf16[64,1536]{1,0:T(8,128)(2,1)S(1)} %collective-permute-done.9.rest_0_, bf16[64,1536]{1,0:T(8,128)(2,1)S(1)} %collective-permute-done.10.rest_1_, f32[8,64,1024]{2,1,0:T(8,128)} %correlate.9.rest_2_), custom_call_target="tpu_custom_call", output_to_operand_aliasing={{}: (3, {})} | custom-call | flops 201326592 | tf_op jit(solution)/shard_map/correlate/pallas_call | solution.py:150
  33.8 1.3 %correlate.11 = f32[8,64,1024]{2,1,0:T(8,128)} custom-call(bf16[512,1536]{1,0:T(8,128)(2,1)S(1)} %modulate.1.modulated, bf16[64,1536]{1,0:T(8,128)(2,1)S(1)} %collective-permute-done.3.rest_0_, bf16[64,1536]{1,0:T(8,128)(2,1)S(1)} %collective-permute-done.4.rest_1_, f32[8,64,1024]{2,1,0:T(8,128)} %correlate.10.rest_2_), custom_call_target="tpu_custom_call", output_to_operand_aliasing={{}: (3, {})} | custom-call | flops 201326592 | tf_op jit(solution)/shard_map/correlate/pallas_call | solution.py:150
  (18 shorter events, 0.5 us)
Async XLA Ops:
  1.3 3.2 %collective-permute-start.5 = (bf16[64,1536]{1,0:T(8,128)(2,1)S(1)}, bf16[64,1536]{1,0:T(8,128)(2,1)S(1)}, u32[]{:S(2)}, u32[]{:S(2)}) collective-permute-start(bf16[64,1536]{1,0:T(8,128)(2,1)S(1)} %whiten.1.white.rest_0_), channel_id=1, source_target_pairs={{0,1},{1,0},{2,3},{3,2},{4,5},{5,4},{6,7},{7,6},{8,9},{9,8},{10,11... | collective-permute-start | bytes 589832 | tf_op jit(solution)/shard_map/ppermute | solution.py:183
  1.8 6.2 %collective-permute-start = (bf16[64,1536]{1,0:T(8,128)(2,1)S(1)}, bf16[64,1536]{1,0:T(8,128)(2,1)S(1)}, u32[]{:S(2)}, u32[]{:S(2)}) collective-permute-start(bf16[64,1536]{1,0:T(8,128)(2,1)S(1)} %whiten.1.white.rest_0_), channel_id=1, source_target_pairs={{0,4},{1,3},{4,8},{5,1},{8,12},{9,5},{12,14},{13,9},{14,10},{15,13... | collective-permute-start | bytes 589832 | tf_op jit(solution)/shard_map/ppermute | solution.py:180
  4.5 5.7 %collective-permute-start.6 = (bf16[64,1536]{1,0:T(8,128)(2,1)S(1)}, bf16[64,1536]{1,0:T(8,128)(2,1)S(1)}, u32[]{:S(2)}, u32[]{:S(2)}) collective-permute-start(bf16[64,1536]{1,0:T(8,128)(2,1)S(1)} %collective-permute-done.5.rest_1_), channel_id=1, source_target_pairs={{0,4},{1,3},{4,8},{5,1},{8,12},{9,5},{12,14},{13,9},{14,10},{15,13... | collective-permute-start | bytes 589832 | tf_op jit(solution)/shard_map/ppermute | solution.py:180
  8.1 5.7 %collective-permute-start.1 = (bf16[64,1536]{1,0:T(8,128)(2,1)S(1)}, bf16[64,1536]{1,0:T(8,128)(2,1)S(1)}, u32[]{:S(2)}, u32[]{:S(2)}) collective-permute-start(bf16[64,1536]{1,0:T(8,128)(2,1)S(1)} %collective-permute-done.rest_0_), channel_id=1, source_target_pairs={{0,4},{1,3},{4,8},{5,1},{8,12},{9,5},{12,14},{13,9},{14,10},{15,13... | collective-permute-start | bytes 589832 | tf_op jit(solution)/shard_map/ppermute | solution.py:180
  10.2 6.2 %collective-permute-start.7 = (bf16[64,1536]{1,0:T(8,128)(2,1)S(1)}, bf16[64,1536]{1,0:T(8,128)(2,1)S(1)}, u32[]{:S(2)}, u32[]{:S(2)}) collective-permute-start(bf16[64,1536]{1,0:T(8,128)(2,1)S(1)} %collective-permute-done.6.rest_1_), channel_id=1, source_target_pairs={{0,4},{1,3},{4,8},{5,1},{8,12},{9,5},{12,14},{13,9},{14,10},{15,13... | collective-permute-start | bytes 589832 | tf_op jit(solution)/shard_map/ppermute | solution.py:180
  13.7 5.7 %collective-permute-start.2 = (bf16[64,1536]{1,0:T(8,128)(2,1)S(1)}, bf16[64,1536]{1,0:T(8,128)(2,1)S(1)}, u32[]{:S(2)}, u32[]{:S(2)}) collective-permute-start(bf16[64,1536]{1,0:T(8,128)(2,1)S(1)} %collective-permute-done.1.rest_0_), channel_id=1, source_target_pairs={{0,4},{1,3},{4,8},{5,1},{8,12},{9,5},{12,14},{13,9},{14,10},{15,13... | collective-permute-start | bytes 589832 | tf_op jit(solution)/shard_map/ppermute | solution.py:180
  15.8 5.7 %collective-permute-start.14 = (bf16[64,1536]{1,0:T(8,128)(2,1)S(1)}, bf16[64,1536]{1,0:T(8,128)(2,1)S(1)}, u32[]{:S(2)}, u32[]{:S(2)}) collective-permute-start(bf16[64,1536]{1,0:T(8,128)(2,1)S(1)} %collective-permute-done.rest_0_), channel_id=1, source_target_pairs={{0,1},{1,0},{2,3},{3,2},{4,5},{5,4},{6,7},{7,6},{8,9},{9,8},{10,11... | collective-permute-start | bytes 589832 | tf_op jit(solution)/shard_map/ppermute | solution.py:183
  15.8 6.2 %collective-permute-start.13 = (bf16[64,1536]{1,0:T(8,128)(2,1)S(1)}, bf16[64,1536]{1,0:T(8,128)(2,1)S(1)}, u32[]{:S(2)}, u32[]{:S(2)}) collective-permute-start(bf16[64,1536]{1,0:T(8,128)(2,1)S(1)} %collective-permute-done.6.rest_1_), channel_id=1, source_target_pairs={{0,1},{1,0},{2,3},{3,2},{4,5},{5,4},{6,7},{7,6},{8,9},{9,8},{10,11... | collective-permute-start | bytes 589832 | tf_op jit(solution)/shard_map/ppermute | solution.py:183
  16.3 5.7 %collective-permute-start.8 = (bf16[64,1536]{1,0:T(8,128)(2,1)S(1)}, bf16[64,1536]{1,0:T(8,128)(2,1)S(1)}, u32[]{:S(2)}, u32[]{:S(2)}) collective-permute-start(bf16[64,1536]{1,0:T(8,128)(2,1)S(1)} %collective-permute-done.7.rest_1_), channel_id=1, source_target_pairs={{0,4},{1,3},{4,8},{5,1},{8,12},{9,5},{12,14},{13,9},{14,10},{15,13... | collective-permute-start | bytes 589832 | tf_op jit(solution)/shard_map/ppermute | solution.py:180
  19.4 5.7 %collective-permute-start.3 = (bf16[64,1536]{1,0:T(8,128)(2,1)S(1)}, bf16[64,1536]{1,0:T(8,128)(2,1)S(1)}, u32[]{:S(2)}, u32[]{:S(2)}) collective-permute-start(bf16[64,1536]{1,0:T(8,128)(2,1)S(1)} %collective-permute-done.2.rest_0_), channel_id=1, source_target_pairs={{0,4},{1,3},{4,8},{5,1},{8,12},{9,5},{12,14},{13,9},{14,10},{15,13... | collective-permute-start | bytes 589832 | tf_op jit(solution)/shard_map/ppermute | solution.py:180
  21.5 9.5 %collective-permute-start.12 = (bf16[64,1536]{1,0:T(8,128)(2,1)S(1)}, bf16[64,1536]{1,0:T(8,128)(2,1)S(1)}, u32[]{:S(2)}, u32[]{:S(2)}) collective-permute-start(bf16[64,1536]{1,0:T(8,128)(2,1)S(1)} %collective-permute-done.1.rest_0_), channel_id=1, source_target_pairs={{0,1},{1,0},{2,3},{3,2},{4,5},{5,4},{6,7},{7,6},{8,9},{9,8},{10,11... | collective-permute-start | bytes 589832 | tf_op jit(solution)/shard_map/ppermute | solution.py:183
  21.5 9.5 %collective-permute-start.11 = (bf16[64,1536]{1,0:T(8,128)(2,1)S(1)}, bf16[64,1536]{1,0:T(8,128)(2,1)S(1)}, u32[]{:S(2)}, u32[]{:S(2)}) collective-permute-start(bf16[64,1536]{1,0:T(8,128)(2,1)S(1)} %collective-permute-done.7.rest_1_), channel_id=1, source_target_pairs={{0,1},{1,0},{2,3},{3,2},{4,5},{5,4},{6,7},{7,6},{8,9},{9,8},{10,11... | collective-permute-start | bytes 589832 | tf_op jit(solution)/shard_map/ppermute | solution.py:183
  22.0 10.5 %collective-permute-start.10 = (bf16[64,1536]{1,0:T(8,128)(2,1)S(1)}, bf16[64,1536]{1,0:T(8,128)(2,1)S(1)}, u32[]{:S(2)}, u32[]{:S(2)}) collective-permute-start(bf16[64,1536]{1,0:T(8,128)(2,1)S(1)} %collective-permute-done.2.rest_0_), channel_id=1, source_target_pairs={{0,1},{1,0},{2,3},{3,2},{4,5},{5,4},{6,7},{7,6},{8,9},{9,8},{10,11... | collective-permute-start | bytes 589832 | tf_op jit(solution)/shard_map/ppermute | solution.py:183
  22.1 10.4 %collective-permute-start.9 = (bf16[64,1536]{1,0:T(8,128)(2,1)S(1)}, bf16[64,1536]{1,0:T(8,128)(2,1)S(1)}, u32[]{:S(2)}, u32[]{:S(2)}) collective-permute-start(bf16[64,1536]{1,0:T(8,128)(2,1)S(1)} %collective-permute-done.8.rest_1_), channel_id=1, source_target_pairs={{0,1},{1,0},{2,3},{3,2},{4,5},{5,4},{6,7},{7,6},{8,9},{9,8},{10,11... | collective-permute-start | bytes 589832 | tf_op jit(solution)/shard_map/ppermute | solution.py:183
  25.1 8.8 %collective-permute-start.4 = (bf16[64,1536]{1,0:T(8,128)(2,1)S(1)}, bf16[64,1536]{1,0:T(8,128)(2,1)S(1)}, u32[]{:S(2)}, u32[]{:S(2)}) collective-permute-start(bf16[64,1536]{1,0:T(8,128)(2,1)S(1)} %collective-permute-done.3.rest_0_), channel_id=1, source_target_pairs={{0,1},{1,0},{2,3},{3,2},{4,5},{5,4},{6,7},{7,6},{8,9},{9,8},{10,11... | collective-permute-start | bytes 589832 | tf_op jit(solution)/shard_map/ppermute | solution.py:183
  25.1 0.7 %copy-start = (f32[8,1,768]{2,1,0:T(1,128)S(1)}, f32[8,1,768]{2,1,0:T(1,128)}, u32[]{:S(2)}) copy-start(f32[8,1,768]{2,1,0:T(1,128)} %constant.4.clone.cosine) | copy-start | bytes 73732
  25.8 0.7 %copy-start.1 = (f32[8,1,768]{2,1,0:T(1,128)S(1)}, f32[8,1,768]{2,1,0:T(1,128)}, u32[]{:S(2)}) copy-start(f32[8,1,768]{2,1,0:T(1,128)} %constant.5.clone.sine) | copy-start | bytes 73732

commit v2 on v1

v2 whole, which is shorter than its diff:
```python
import math

import numpy as np
import jax
import jax.numpy as jnp
from jax import lax
from jax.experimental import pallas as pl
from jax.experimental.pallas import tpu as pltpu
from jax.sharding import PartitionSpec as P


LAGS = 8

level_floor = 0.3
first_bin = 96.0
REACH = 2
ROOM = 16 * 2**20
PARTS = 2


def phase_tables(bin_count, win_count, lag_count):
    freq = first_bin + np.arange(bin_count, dtype=np.float64)
    shifts = 3.0 + 5.0 * np.arange(lag_count, dtype=np.float64)
    theta = 2.0 * math.pi * shifts[:, None] * freq[None, :] / 512.0
    scale = 1.0 / math.sqrt(win_count * bin_count)
    tables = [np.tile(part(theta) * scale, (1, win_count)) for part in (np.cos, np.sin)]
    return jnp.asarray(np.concatenate(tables), jnp.float32)


def near(array):
    return pltpu.with_memory_space_constraint(array, pltpu.VMEM)


def far(array):
    return pltpu.with_memory_space_constraint(array, pltpu.HBM)


def whiten_body(spectra, gap_mask, tables, out, tables_near):
    tables_near[...] = tables[...]
    wide = spectra.shape[2]
    bin_count = wide // gap_mask.shape[0]
    real = spectra[0].astype(jnp.float32)
    imag = spectra[1].astype(jnp.float32)
    amplitude = jnp.sqrt(real * real + imag * imag)
    lane = lax.broadcasted_iota(jnp.int32, amplitude.shape, 1) % bin_count
    total = amplitude
    count = jnp.ones(amplitude.shape, jnp.float32)
    for step in range(1, REACH + 1):
        above = lane + step < bin_count
        below = lane >= step
        total = total + jnp.where(above, pltpu.roll(amplitude, wide - step, 1), 0.0)
        total = total + jnp.where(below, pltpu.roll(amplitude, step, 1), 0.0)
        count = count + above.astype(jnp.float32) + below.astype(jnp.float32)
    level = jnp.maximum(total / count, level_floor)
    window = lax.broadcasted_iota(jnp.int32, (gap_mask.shape[0], wide), 1) // bin_count
    spread = window == lax.broadcasted_iota(jnp.int32, window.shape, 0)
    kept = lax.dot_general(
        gap_mask[...].astype(jnp.float32).astype(jnp.bfloat16),
        spread.astype(jnp.float32).astype(jnp.bfloat16),
        (((0,), (0,)), ((), ())),
        preferred_element_type=jnp.float32,
    )
    factor = kept / level
    out[:, :wide] = (real * factor).astype(jnp.bfloat16)
    out[:, wide:] = (imag * factor).astype(jnp.bfloat16)


def whiten(spectra, gap_mask):
    members, wide = spectra.shape[1:]
    win_count = gap_mask.shape[1]
    tables = phase_tables(wide // win_count, win_count, LAGS)
    return pl.pallas_call(
        whiten_body,
        out_shape=[
            pltpu.VMEM((members, 2 * wide), jnp.bfloat16),
            pltpu.VMEM(tables.shape, jnp.float32),
        ],
        compiler_params=pltpu.CompilerParams(vmem_limit_bytes=ROOM),
        name="whiten",
    )(far(spectra), far(gap_mask.T), far(tables))


def modulate_body(white, tables, out):
    members = white.shape[0]
    wide = white.shape[1] // 2
    real = white[:, :wide].astype(jnp.float32)
    imag = white[:, wide:].astype(jnp.float32)
    lags = tables.shape[0] // 2
    for lag in range(lags):
        rows = slice(lag * members, (lag + 1) * members)
        c = tables[lag : lag + 1, :]
        s = tables[lags + lag : lags + lag + 1, :]
        out[rows, :wide] = (c * real - s * imag).astype(jnp.bfloat16)
        out[rows, wide:] = (c * imag + s * real).astype(jnp.bfloat16)


def modulate(white, tables):
    members = white.shape[0]
    return pl.pallas_call(
        modulate_body,
        out_shape=pltpu.VMEM((LAGS * members, white.shape[1]), jnp.bfloat16),
        compiler_params=pltpu.CompilerParams(vmem_limit_bytes=ROOM),
        cost_estimate=pl.CostEstimate(flops=12 * LAGS * white.size, bytes_accessed=0, transcendentals=0),
        name="modulate",
    )(near(white), near(tables))


def walk_at(seat, chips):
    return jnp.where(seat < chips // 2, 2 * seat, 2 * (chips - 1 - seat) + 1)


def seat_of(chip, chips):
    return jnp.where(chip % 2 == 0, chip // 2, chips - 1 - chip // 2)


def correlate(modulated, groups, chips, shape, before, end):
    members = shape[1]
    count = len(groups)
    flat = [piece for _, mine, other in groups for piece in (mine, other)]
    old_groups, old_tiles, onto = before if before else ([], None, None)
    olds = ([] if old_tiles is None else [old_tiles]) + ([] if onto is None else [onto])

    def body(modulated, *rest):
        pieces = rest[: len(flat)]
        old_tile = rest[len(flat)]
        tail = rest[len(flat) + len(olds) :]
        if end:
            out, block, sems, tile = tail
        elif old_groups:
            tile, out, block, sems = tail
        else:
            tile, block, sems = tail
        place = lax.axis_index("blk")
        core = lax.rem(place, 2)
        seat = seat_of(lax.div(place, 2), chips)
        copies = []

        def send(source, back, some, sem):
            home = walk_at(lax.rem(seat + chips - back * (1 - 2 * core), chips), chips)
            columns = pl.ds(pl.multiple_of(home * (2 * members), 2 * members), 2 * members)
            copy = pltpu.make_async_copy(source, out.at[some, :, columns], sem)
            copy.start()
            copies.append(copy)

        for g, (back, _, _) in enumerate(old_groups):
            send(old_tile.at[g], back, slice(None), sems.at[g, PARTS])
        for g in range(count):
            for side, piece in ((core, pieces[2 * g]), (1 - core, pieces[2 * g + 1])):
                rows = pl.ds(pl.multiple_of((2 * g + side) * members, members), members)
                block[rows, :] = piece[...]
        parts = PARTS if end else 1
        lags = shape[0] // parts
        for part in range(parts):
            some = pl.ds(part * lags, lags)
            sums = lax.dot_general(
                modulated[part * lags * members : (part + 1) * lags * members, :],
                block[...],
                (((1,), (1,)), ((), ())),
                preferred_element_type=jnp.float32,
            ).reshape(lags, members, 2 * count * members)
            for g, (back, _, _) in enumerate(groups):
                tile[g, some] = sums[:, :, 2 * g * members : 2 * (g + 1) * members]
                if end:
                    send(tile.at[g, some], back, some, sems.at[g, part])
        for copy in copies:
            copy.wait()

    vmem = pl.BlockSpec(memory_space=pltpu.VMEM)
    anywhere = pl.BlockSpec(memory_space=pl.ANY)
    tile_shape = (count, shape[0], members, 2 * members)
    outs = [] if end else [(pltpu.VMEM(tile_shape, jnp.float32), vmem)]
    if old_groups:
        outs.append((jax.ShapeDtypeStruct(shape, jnp.float32), anywhere))
    scratch = [
        pltpu.VMEM((count * 2 * members, modulated.shape[1]), jnp.bfloat16),
        pltpu.SemaphoreType.DMA((max(count, len(old_groups)), PARTS + 1)),
    ]
    got = pl.pallas_call(
        body,
        out_shape=[shaped for shaped, _ in outs],
        in_specs=[vmem] * (1 + len(flat)) + [vmem] * (old_tiles is not None) + [anywhere] * (onto is not None),
        out_specs=[spec for _, spec in outs],
        scratch_shapes=scratch + ([pltpu.VMEM(tile_shape, jnp.float32)] if end else []),
        input_output_aliases={} if onto is None else {2 + len(flat): len(outs) - 1},
        compiler_params=pltpu.CompilerParams(vmem_limit_bytes=ROOM),
        cost_estimate=pl.CostEstimate(
            flops=4 * count * members * modulated.size, bytes_accessed=0, transcendentals=0
        ),
        name="correlate",
    )(
        near(modulated),
        *[near(piece) for piece in flat],
        *([] if old_tiles is None else [near(old_tiles)]),
        *([] if onto is None else [onto]),
    )
    if end:
        return got[0]
    return groups, got[0], got[1] if old_groups else None


def per_device(spectra, gap_mask):
    devices = lax.axis_size("blk")
    chips = devices // 2
    walk = list(range(0, chips, 2)) + list(range(1, chips, 2))[::-1]
    members = spectra.shape[1]
    shape = (LAGS, members, devices * members)

    def onward(array, step):
        pairs = [
            (2 * walk[i] + (c + step + 1) % 2, 2 * walk[(i + 1 - 2 * c) % chips] + (c + step) % 2)
            for i in range(chips)
            for c in range(2)
        ]
        return lax.ppermute(array, "blk", pairs)

    def swap(array):
        return lax.ppermute(array, "blk", [(i, i ^ 1) for i in range(devices)])

    def add(groups, before, end=False):
        return correlate(modulated, groups, chips, shape, before, end)

    white, tables = whiten(spectra, gap_mask)
    modulated = modulate(white, tables)

    mine, other = white, swap(white)
    out = add([(0, mine, other)], None)
    final = chips // 2
    for step in range(1, final):
        mine = onward(mine, step)
        other = onward(other, step)
        mine_there, other_there = swap(mine), swap(other)
        if step % 2:
            groups = [(-step, other, mine), (step, mine_there, other_there)]
        else:
            groups = [(step, mine, other), (-step, other_there, mine_there)]
        out = add(groups, out)
    last = onward(mine, final)
    there = swap(last)
    return add([(final, there, last) if final % 2 else (final, last, there)], out, end=True)


def solution(mesh):
    placed = (P(None, ("group", "blk"), None), P(("group", "blk"), None))
    return jax.shard_map(
        per_device,
        mesh=mesh,
        in_specs=placed,
        out_specs=P(None, ("group", "blk"), None),
        check_vma=False,
    )
```

time: 35.4 us -> 30.6 us (0.86)
  Pallas kernels: 9.77 us -> 7.56 us
  local copies, waits for them, and re-layouts: 1.47 us -> 0 us
  starting transfers between devices: 16.2 us -> 15 us
    pallas_call x7 -> x6, Pallas kernels: 9.39 us -> 7.17 us  [the longest x5 5.87 us: correlate(): pl.pallas_call(body, out_shape=[shaped for shaped, _ in outs], in_specs=[...]
    unnamed x4 -> x0, local copies, waits for them, and re-layouts: 1.47 us -> none
    ppermute x7, starting transfers between devices: 14.1 us -> 12.8 us  [onward(): return lax.ppermute(array, 'blk', pairs)]
  transfers between devices with their start and end apart: 15 -> 15, of which waited for: 4 -> 5; matrix products, arithmetic and copies ran while one was open for 0% -> 0% of each run, Pallas kernels for 20% -> 16%
where the time goes in v2:
time: 30.6 us; the launch traced here: 30.5 us
  starting transfers between devices  15 us (49%)
  waiting for transfers between devices  7.83 us (26%)
  Pallas kernels  7.56 us (25%)
    ppermute x7, starting transfers between devices, onward(): return lax.ppermute(array, 'blk', pairs)  12.8 us
    ppermute x7, waiting for transfers between devices, onward(): return lax.ppermute(array, 'blk', pairs)  7.81 us
    pallas_call x5, Pallas kernels, correlate(): pl.pallas_call(body, out_shape=[shaped for shaped, _ in outs], in_specs=[...  5.87 us
    ppermute x8, starting transfers between devices, swap(): return lax.ppermute(array, 'blk', [(i, i ^ 1) for i in range(devices)])  2.2 us
    pallas_call x1, Pallas kernels, whiten(): pl.pallas_call(whiten_body, out_shape=[pltpu.VMEM((members, 2 * wide), jn...  1.29 us
  transfers between devices with their start and end apart: 15, of which 5 were waited for; matrix products, arithmetic and copies ran while one was open for 0% of the time, Pallas kernels for 16%

profile of v2, /device:TPU:0, one launch (start us, length us, event | category | flops | bytes accessed | tf_op | source)
XLA Modules:
  0.0 30.5 jit_solution(321226694773131003)
XLA Ops:
  0.0 1.3 %whiten.1 = (bf16[64,1536]{1,0:T(8,128)(2,1)S(1)}, f32[16,768]{1,0:T(8,128)S(1)}) custom-call(bf16[2,64,768]{2,1,0:T(8,128)(2,1)} %spectra.1, s32[48,64]{1,0:T(8,128)} %bitcast.1, f32[16,768]{1,0:T(8,128)} %constant.2.clone.tables), custom_call_target="tpu_custom_call" | custom-call | tf_op jit(solution)/shard_map/whiten/pallas_call | solution.py:72
  1.3 0.6 %collective-permute-start.5 = (bf16[64,1536]{1,0:T(8,128)(2,1)S(1)}, bf16[64,1536]{1,0:T(8,128)(2,1)S(1)}, u32[]{:S(2)}, u32[]{:S(2)}) collective-permute-start(bf16[64,1536]{1,0:T(8,128)(2,1)S(1)} %get-tuple-element.13.white.rest_0_), channel_id=1, source_target_pairs={{0,1},{1,0},{2,3},{3,2},{4,5},{5,4},{6,7},{7,6},{8,9},{9,8},{10,11... | collective-permute-start | bytes 589832 | tf_op jit(solution)/shard_map/ppermute | solution.py:217
  1.9 2.7 %collective-permute-start = (bf16[64,1536]{1,0:T(8,128)(2,1)S(1)}, bf16[64,1536]{1,0:T(8,128)(2,1)S(1)}, u32[]{:S(2)}, u32[]{:S(2)}) collective-permute-start(bf16[64,1536]{1,0:T(8,128)(2,1)S(1)} %get-tuple-element.13.white.rest_0_), channel_id=1, source_target_pairs={{0,5},{1,2},{4,9},{5,0},{8,13},{9,4},{12,15},{13,8},{14,11},{15,12... | collective-permute-start | bytes 589832 | tf_op jit(solution)/shard_map/ppermute | solution.py:214
  4.5 1.1 %collective-permute-start.6 = (bf16[64,1536]{1,0:T(8,128)(2,1)S(1)}, bf16[64,1536]{1,0:T(8,128)(2,1)S(1)}, u32[]{:S(2)}, u32[]{:S(2)}) collective-permute-start(bf16[64,1536]{1,0:T(8,128)(2,1)S(1)} %collective-permute-done.5.rest_1_), channel_id=1, source_target_pairs={{0,5},{1,2},{4,9},{5,0},{8,13},{9,4},{12,15},{13,8},{14,11},{15,12... | collective-permute-start | bytes 589832 | tf_op jit(solution)/shard_map/ppermute | solution.py:214
  5.6 2.3 %collective-permute-done.rest_1_ = bf16[64,1536]{1,0:T(8,128)(2,1)S(1)} collective-permute-done((bf16[64,1536]{1,0:T(8,128)(2,1)S(1)}, bf16[64,1536]{1,0:T(8,128)(2,1)S(1)}, u32[]{:S(2)}, u32[]{:S(2)}) %collective-permute-start) | collective-permute-done | bytes 196640 | tf_op jit(solution)/shard_map/ppermute | solution.py:214
  7.9 2.0 %collective-permute-start.1 = (bf16[64,1536]{1,0:T(8,128)(2,1)S(1)}, bf16[64,1536]{1,0:T(8,128)(2,1)S(1)}, u32[]{:S(2)}, u32[]{:S(2)}) collective-permute-start(bf16[64,1536]{1,0:T(8,128)(2,1)S(1)} %collective-permute-done.rest_1_), channel_id=1, source_target_pairs={{1,4},{0,3},{5,8},{4,1},{9,12},{8,5},{13,14},{12,9},{15,10},{14,13... | collective-permute-start | bytes 589832 | tf_op jit(solution)/shard_map/ppermute | solution.py:214
  9.9 0.1 collective-permute-done.6.rest_0_
  10.0 1.7 %collective-permute-start.7 = (bf16[64,1536]{1,0:T(8,128)(2,1)S(1)}, bf16[64,1536]{1,0:T(8,128)(2,1)S(1)}, u32[]{:S(2)}, u32[]{:S(2)}) collective-permute-start(bf16[64,1536]{1,0:T(8,128)(2,1)S(1)} %collective-permute-done.6.rest_0_), channel_id=1, source_target_pairs={{1,4},{0,3},{5,8},{4,1},{9,12},{8,5},{13,14},{12,9},{15,10},{14,13... | collective-permute-start | bytes 589832 | tf_op jit(solution)/shard_map/ppermute | solution.py:214
  11.7 1.5 %collective-permute-done.1.rest_0_ = bf16[64,1536]{1,0:T(8,128)(2,1)S(1)} collective-permute-done((bf16[64,1536]{1,0:T(8,128)(2,1)S(1)}, bf16[64,1536]{1,0:T(8,128)(2,1)S(1)}, u32[]{:S(2)}, u32[]{:S(2)}) %collective-permute-start.1) | collective-permute-done | bytes 196640 | tf_op jit(solution)/shard_map/ppermute | solution.py:214
  13.2 2.1 %collective-permute-start.2 = (bf16[64,1536]{1,0:T(8,128)(2,1)S(1)}, bf16[64,1536]{1,0:T(8,128)(2,1)S(1)}, u32[]{:S(2)}, u32[]{:S(2)}) collective-permute-start(bf16[64,1536]{1,0:T(8,128)(2,1)S(1)} %collective-permute-done.1.rest_0_), channel_id=1, source_target_pairs={{0,5},{1,2},{4,9},{5,0},{8,13},{9,4},{12,15},{13,8},{14,11},{15,12... | collective-permute-start | bytes 589832 | tf_op jit(solution)/shard_map/ppermute | solution.py:214
  15.3 0.5 %collective-permute-start.14 = (bf16[64,1536]{1,0:T(8,128)(2,1)S(1)}, bf16[64,1536]{1,0:T(8,128)(2,1)S(1)}, u32[]{:S(2)}, u32[]{:S(2)}) collective-permute-start(bf16[64,1536]{1,0:T(8,128)(2,1)S(1)} %collective-permute-done.6.rest_0_), channel_id=1, source_target_pairs={{0,1},{1,0},{2,3},{3,2},{4,5},{5,4},{6,7},{7,6},{8,9},{9,8},{10,11... | collective-permute-start | bytes 589832 | tf_op jit(solution)/shard_map/ppermute | solution.py:217
  15.8 1.3 %collective-permute-start.8 = (bf16[64,1536]{1,0:T(8,128)(2,1)S(1)}, bf16[64,1536]{1,0:T(8,128)(2,1)S(1)}, u32[]{:S(2)}, u32[]{:S(2)}) collective-permute-start(bf16[64,1536]{1,0:T(8,128)(2,1)S(1)} %collective-permute-done.7.rest_1_), channel_id=1, source_target_pairs={{0,5},{1,2},{4,9},{5,0},{8,13},{9,4},{12,15},{13,8},{14,11},{15,12... | collective-permute-start | bytes 589832 | tf_op jit(solution)/shard_map/ppermute | solution.py:214
  17.1 1.5 %collective-permute-done.2.rest_1_ = bf16[64,1536]{1,0:T(8,128)(2,1)S(1)} collective-permute-done((bf16[64,1536]{1,0:T(8,128)(2,1)S(1)}, bf16[64,1536]{1,0:T(8,128)(2,1)S(1)}, u32[]{:S(2)}, u32[]{:S(2)}) %collective-permute-start.2) | collective-permute-done | bytes 196640 | tf_op jit(solution)/shard_map/ppermute | solution.py:214
  18.7 2.0 %collective-permute-start.3 = (bf16[64,1536]{1,0:T(8,128)(2,1)S(1)}, bf16[64,1536]{1,0:T(8,128)(2,1)S(1)}, u32[]{:S(2)}, u32[]{:S(2)}) collective-permute-start(bf16[64,1536]{1,0:T(8,128)(2,1)S(1)} %collective-permute-done.2.rest_1_), channel_id=1, source_target_pairs={{1,4},{0,3},{5,8},{4,1},{9,12},{8,5},{13,14},{12,9},{15,10},{14,13... | collective-permute-start | bytes 589832 | tf_op jit(solution)/shard_map/ppermute | solution.py:214
  20.7 0.5 %collective-permute-start.11 = (bf16[64,1536]{1,0:T(8,128)(2,1)S(1)}, bf16[64,1536]{1,0:T(8,128)(2,1)S(1)}, u32[]{:S(2)}, u32[]{:S(2)}) collective-permute-start(bf16[64,1536]{1,0:T(8,128)(2,1)S(1)} %collective-permute-done.7.rest_1_), channel_id=1, source_target_pairs={{0,1},{1,0},{2,3},{3,2},{4,5},{5,4},{6,7},{7,6},{8,9},{9,8},{10,11... | collective-permute-start | bytes 589832 | tf_op jit(solution)/shard_map/ppermute | solution.py:217
  21.2 0.4 %collective-permute-start.10 = (bf16[64,1536]{1,0:T(8,128)(2,1)S(1)}, bf16[64,1536]{1,0:T(8,128)(2,1)S(1)}, u32[]{:S(2)}, u32[]{:S(2)}) collective-permute-start(bf16[64,1536]{1,0:T(8,128)(2,1)S(1)} %collective-permute-done.8.rest_0_), channel_id=1, source_target_pairs={{0,1},{1,0},{2,3},{3,2},{4,5},{5,4},{6,7},{7,6},{8,9},{9,8},{10,11... | collective-permute-start | bytes 589832 | tf_op jit(solution)/shard_map/ppermute | solution.py:217
  21.7 2.3 %collective-permute-done.3.rest_0_ = bf16[64,1536]{1,0:T(8,128)(2,1)S(1)} collective-permute-done((bf16[64,1536]{1,0:T(8,128)(2,1)S(1)}, bf16[64,1536]{1,0:T(8,128)(2,1)S(1)}, u32[]{:S(2)}, u32[]{:S(2)}) %collective-permute-start.3) | collective-permute-done | bytes 196640 | tf_op jit(solution)/shard_map/ppermute | solution.py:214
  24.0 0.1 collective-permute-start.4
  24.1 0.4 %modulate.1.modulated = bf16[512,1536]{1,0:T(8,128)(2,1)S(1)} custom-call(bf16[64,1536]{1,0:T(8,128)(2,1)S(1)} %get-tuple-element.13.white.rest_0_, f32[16,768]{1,0:T(8,128)S(1)} %get-tuple-element.14.tables), custom_call_target="tpu_custom_call" | custom-call | flops 9437184 | tf_op jit(solution)/shard_map/modulate/pallas_call | solution.py:99
  24.5 0.6 %correlate.5.rest_4_ = f32[1,8,64,128]{3,2,1,0:T(8,128)S(1)} custom-call(bf16[512,1536]{1,0:T(8,128)(2,1)S(1)} %modulate.1.modulated, bf16[64,1536]{1,0:T(8,128)(2,1)S(1)} %get-tuple-element.13.white.rest_0_, bf16[64,1536]{1,0:T(8,128)(2,1)S(1)} %collective-permute-done.5.rest_1_), custom_call_target="tpu_custom_call" | custom-call | flops 201326592 | tf_op jit(solution)/shard_map/correlate/pallas_call | solution.py:178
  25.1 1.3 %correlate.6 = (f32[2,8,64,128]{3,2,1,0:T(8,128)S(1)}, f32[8,64,1024]{2,1,0:T(8,128)}) custom-call(bf16[512,1536]{1,0:T(8,128)(2,1)S(1)} %modulate.1.modulated, bf16[64,1536]{1,0:T(8,128)(2,1)S(1)} %collective-permute-done.6.rest_0_, bf16[64,1536]{1,0:T(8,128)(2,1)S(1)} %collective-permute-done.rest_1_, ...), custom_call_target="tpu_custom_call" | custom-call | flops 402653184 | tf_op jit(solution)/shard_map/correlate/pallas_call | solution.py:178
  26.4 1.4 %correlate.7 = (f32[2,8,64,128]{3,2,1,0:T(8,128)S(1)}, f32[8,64,1024]{2,1,0:T(8,128)}) custom-call(bf16[512,1536]{1,0:T(8,128)(2,1)S(1)} %modulate.1.modulated, bf16[64,1536]{1,0:T(8,128)(2,1)S(1)} %collective-permute-done.1.rest_0_, bf16[64,1536]{1,0:T(8,128)(2,1)S(1)} %collective-permute-done.7.rest_1_, ...), custom_call_target="tpu_custom_call", output_to_operand_aliasing={{1}: (6, {})} | custom-call | flops 402653184 | tf_op jit(solution)/shard_map/correlate/pallas_call | solution.py:178
  27.8 1.3 %correlate.8 = (f32[2,8,64,128]{3,2,1,0:T(8,128)S(1)}, f32[8,64,1024]{2,1,0:T(8,128)}) custom-call(bf16[512,1536]{1,0:T(8,128)(2,1)S(1)} %modulate.1.modulated, bf16[64,1536]{1,0:T(8,128)(2,1)S(1)} %collective-permute-done.8.rest_0_, bf16[64,1536]{1,0:T(8,128)(2,1)S(1)} %collective-permute-done.2.rest_1_, ...), custom_call_target="tpu_custom_call", output_to_operand_aliasing={{1}: (6, {})} | custom-call | flops 402653184 | tf_op jit(solution)/shard_map/correlate/pallas_call | solution.py:178
  29.1 1.3 %correlate.9 = f32[8,64,1024]{2,1,0:T(8,128)} custom-call(bf16[512,1536]{1,0:T(8,128)(2,1)S(1)} %modulate.1.modulated, bf16[64,1536]{1,0:T(8,128)(2,1)S(1)} %collective-permute-done.3.rest_0_, bf16[64,1536]{1,0:T(8,128)(2,1)S(1)} %collective-permute-done.4.rest_1_, f32[2,8,64,128]{3,2,1,0:T(8,128)S(1)} %get-tuple-element.19.rest_2_, ...), custom_call_target="tpu_custom_call", output_to_operand_aliasing={{}: (4, {})} | custom-call | flops 201326592 | tf_op jit(solution)/shard_map/correlate/pallas_call | solution.py:178
  (13 shorter events, 0.1 us)
Async XLA Ops:
  1.3 3.2 %collective-permute-start.5 = (bf16[64,1536]{1,0:T(8,128)(2,1)S(1)}, bf16[64,1536]{1,0:T(8,128)(2,1)S(1)}, u32[]{:S(2)}, u32[]{:S(2)}) collective-permute-start(bf16[64,1536]{1,0:T(8,128)(2,1)S(1)} %get-tuple-element.13.white.rest_0_), channel_id=1, source_target_pairs={{0,1},{1,0},{2,3},{3,2},{4,5},{5,4},{6,7},{7,6},{8,9},{9,8},{10,11... | collective-permute-start | bytes 589832 | tf_op jit(solution)/shard_map/ppermute | solution.py:217
  1.9 6.0 %collective-permute-start = (bf16[64,1536]{1,0:T(8,128)(2,1)S(1)}, bf16[64,1536]{1,0:T(8,128)(2,1)S(1)}, u32[]{:S(2)}, u32[]{:S(2)}) collective-permute-start(bf16[64,1536]{1,0:T(8,128)(2,1)S(1)} %get-tuple-element.13.white.rest_0_), channel_id=1, source_target_pairs={{0,5},{1,2},{4,9},{5,0},{8,13},{9,4},{12,15},{13,8},{14,11},{15,12... | collective-permute-start | bytes 589832 | tf_op jit(solution)/shard_map/ppermute | solution.py:214
  4.5 5.5 %collective-permute-start.6 = (bf16[64,1536]{1,0:T(8,128)(2,1)S(1)}, bf16[64,1536]{1,0:T(8,128)(2,1)S(1)}, u32[]{:S(2)}, u32[]{:S(2)}) collective-permute-start(bf16[64,1536]{1,0:T(8,128)(2,1)S(1)} %collective-permute-done.5.rest_1_), channel_id=1, source_target_pairs={{0,5},{1,2},{4,9},{5,0},{8,13},{9,4},{12,15},{13,8},{14,11},{15,12... | collective-permute-start | bytes 589832 | tf_op jit(solution)/shard_map/ppermute | solution.py:214
  7.9 5.3 %collective-permute-start.1 = (bf16[64,1536]{1,0:T(8,128)(2,1)S(1)}, bf16[64,1536]{1,0:T(8,128)(2,1)S(1)}, u32[]{:S(2)}, u32[]{:S(2)}) collective-permute-start(bf16[64,1536]{1,0:T(8,128)(2,1)S(1)} %collective-permute-done.rest_1_), channel_id=1, source_target_pairs={{1,4},{0,3},{5,8},{4,1},{9,12},{8,5},{13,14},{12,9},{15,10},{14,13... | collective-permute-start | bytes 589832 | tf_op jit(solution)/shard_map/ppermute | solution.py:214
  10.0 5.8 %collective-permute-start.7 = (bf16[64,1536]{1,0:T(8,128)(2,1)S(1)}, bf16[64,1536]{1,0:T(8,128)(2,1)S(1)}, u32[]{:S(2)}, u32[]{:S(2)}) collective-permute-start(bf16[64,1536]{1,0:T(8,128)(2,1)S(1)} %collective-permute-done.6.rest_0_), channel_id=1, source_target_pairs={{1,4},{0,3},{5,8},{4,1},{9,12},{8,5},{13,14},{12,9},{15,10},{14,13... | collective-permute-start | bytes 589832 | tf_op jit(solution)/shard_map/ppermute | solution.py:214
  13.2 5.4 %collective-permute-start.2 = (bf16[64,1536]{1,0:T(8,128)(2,1)S(1)}, bf16[64,1536]{1,0:T(8,128)(2,1)S(1)}, u32[]{:S(2)}, u32[]{:S(2)}) collective-permute-start(bf16[64,1536]{1,0:T(8,128)(2,1)S(1)} %collective-permute-done.1.rest_0_), channel_id=1, source_target_pairs={{0,5},{1,2},{4,9},{5,0},{8,13},{9,4},{12,15},{13,8},{14,11},{15,12... | collective-permute-start | bytes 589832 | tf_op jit(solution)/shard_map/ppermute | solution.py:214
  15.3 5.3 %collective-permute-start.13 = (bf16[64,1536]{1,0:T(8,128)(2,1)S(1)}, bf16[64,1536]{1,0:T(8,128)(2,1)S(1)}, u32[]{:S(2)}, u32[]{:S(2)}) collective-permute-start(bf16[64,1536]{1,0:T(8,128)(2,1)S(1)} %collective-permute-done.rest_1_), channel_id=1, source_target_pairs={{0,1},{1,0},{2,3},{3,2},{4,5},{5,4},{6,7},{7,6},{8,9},{9,8},{10,11... | collective-permute-start | bytes 589832 | tf_op jit(solution)/shard_map/ppermute | solution.py:217
  15.3 5.8 %collective-permute-start.14 = (bf16[64,1536]{1,0:T(8,128)(2,1)S(1)}, bf16[64,1536]{1,0:T(8,128)(2,1)S(1)}, u32[]{:S(2)}, u32[]{:S(2)}) collective-permute-start(bf16[64,1536]{1,0:T(8,128)(2,1)S(1)} %collective-permute-done.6.rest_0_), channel_id=1, source_target_pairs={{0,1},{1,0},{2,3},{3,2},{4,5},{5,4},{6,7},{7,6},{8,9},{9,8},{10,11... | collective-permute-start | bytes 589832 | tf_op jit(solution)/shard_map/ppermute | solution.py:217
  15.8 5.4 %collective-permute-start.8 = (bf16[64,1536]{1,0:T(8,128)(2,1)S(1)}, bf16[64,1536]{1,0:T(8,128)(2,1)S(1)}, u32[]{:S(2)}, u32[]{:S(2)}) collective-permute-start(bf16[64,1536]{1,0:T(8,128)(2,1)S(1)} %collective-permute-done.7.rest_1_), channel_id=1, source_target_pairs={{0,5},{1,2},{4,9},{5,0},{8,13},{9,4},{12,15},{13,8},{14,11},{15,12... | collective-permute-start | bytes 589832 | tf_op jit(solution)/shard_map/ppermute | solution.py:214
  18.7 5.3 %collective-permute-start.3 = (bf16[64,1536]{1,0:T(8,128)(2,1)S(1)}, bf16[64,1536]{1,0:T(8,128)(2,1)S(1)}, u32[]{:S(2)}, u32[]{:S(2)}) collective-permute-start(bf16[64,1536]{1,0:T(8,128)(2,1)S(1)} %collective-permute-done.2.rest_1_), channel_id=1, source_target_pairs={{1,4},{0,3},{5,8},{4,1},{9,12},{8,5},{13,14},{12,9},{15,10},{14,13... | collective-permute-start | bytes 589832 | tf_op jit(solution)/shard_map/ppermute | solution.py:214
  20.6 5.8 %collective-permute-start.12 = (bf16[64,1536]{1,0:T(8,128)(2,1)S(1)}, bf16[64,1536]{1,0:T(8,128)(2,1)S(1)}, u32[]{:S(2)}, u32[]{:S(2)}) collective-permute-start(bf16[64,1536]{1,0:T(8,128)(2,1)S(1)} %collective-permute-done.1.rest_0_), channel_id=1, source_target_pairs={{0,1},{1,0},{2,3},{3,2},{4,5},{5,4},{6,7},{7,6},{8,9},{9,8},{10,11... | collective-permute-start | bytes 589832 | tf_op jit(solution)/shard_map/ppermute | solution.py:217
  20.7 5.8 %collective-permute-start.11 = (bf16[64,1536]{1,0:T(8,128)(2,1)S(1)}, bf16[64,1536]{1,0:T(8,128)(2,1)S(1)}, u32[]{:S(2)}, u32[]{:S(2)}) collective-permute-start(bf16[64,1536]{1,0:T(8,128)(2,1)S(1)} %collective-permute-done.7.rest_1_), channel_id=1, source_target_pairs={{0,1},{1,0},{2,3},{3,2},{4,5},{5,4},{6,7},{7,6},{8,9},{9,8},{10,11... | collective-permute-start | bytes 589832 | tf_op jit(solution)/shard_map/ppermute | solution.py:217
  21.2 6.7 %collective-permute-start.9 = (bf16[64,1536]{1,0:T(8,128)(2,1)S(1)}, bf16[64,1536]{1,0:T(8,128)(2,1)S(1)}, u32[]{:S(2)}, u32[]{:S(2)}) collective-permute-start(bf16[64,1536]{1,0:T(8,128)(2,1)S(1)} %collective-permute-done.2.rest_1_), channel_id=1, source_target_pairs={{0,1},{1,0},{2,3},{3,2},{4,5},{5,4},{6,7},{7,6},{8,9},{9,8},{10,11... | collective-permute-start | bytes 589832 | tf_op jit(solution)/shard_map/ppermute | solution.py:217
  21.2 6.6 %collective-permute-start.10 = (bf16[64,1536]{1,0:T(8,128)(2,1)S(1)}, bf16[64,1536]{1,0:T(8,128)(2,1)S(1)}, u32[]{:S(2)}, u32[]{:S(2)}) collective-permute-start(bf16[64,1536]{1,0:T(8,128)(2,1)S(1)} %collective-permute-done.8.rest_0_), channel_id=1, source_target_pairs={{0,1},{1,0},{2,3},{3,2},{4,5},{5,4},{6,7},{7,6},{8,9},{9,8},{10,11... | collective-permute-start | bytes 589832 | tf_op jit(solution)/shard_map/ppermute | solution.py:217
  24.0 5.1 %collective-permute-start.4 = (bf16[64,1536]{1,0:T(8,128)(2,1)S(1)}, bf16[64,1536]{1,0:T(8,128)(2,1)S(1)}, u32[]{:S(2)}, u32[]{:S(2)}) collective-permute-start(bf16[64,1536]{1,0:T(8,128)(2,1)S(1)} %collective-permute-done.3.rest_0_), channel_id=1, source_target_pairs={{0,1},{1,0},{2,3},{3,2},{4,5},{5,4},{6,7},{7,6},{8,9},{9,8},{10,11... | collective-permute-start | bytes 589832 | tf_op jit(solution)/shard_map/ppermute | solution.py:217

commit v3 on v2

--- a/solution.py
+++ b/solution.py
@@ -113,20 +113,20 @@
     return jnp.where(chip % 2 == 0, chip // 2, chips - 1 - chip // 2)
 
 
-def correlate(modulated, groups, chips, shape, before, end):
+def correlate(modulated, groups, chips, shape, old=(), onto=None, end=False):
     members = shape[1]
     count = len(groups)
     flat = [piece for _, mine, other in groups for piece in (mine, other)]
-    old_groups, old_tiles, onto = before if before else ([], None, None)
-    olds = ([] if old_tiles is None else [old_tiles]) + ([] if onto is None else [onto])
+    old_tiles = [tiles for _, tiles in old]
+    first_onto = 1 + len(flat) + len(old_tiles)
 
     def body(modulated, *rest):
         pieces = rest[: len(flat)]
-        old_tile = rest[len(flat)]
-        tail = rest[len(flat) + len(olds) :]
+        old_refs = rest[len(flat) : len(flat) + len(old)]
+        tail = rest[len(flat) + len(old) + (onto is not None) :]
         if end:
             out, block, sems, tile = tail
-        elif old_groups:
+        elif old:
             tile, out, block, sems = tail
         else:
             tile, block, sems = tail
@@ -135,15 +135,16 @@
         seat = seat_of(lax.div(place, 2), chips)
         copies = []
 
-        def send(source, back, some, sem):
+        def send(source, back, some):
             home = walk_at(lax.rem(seat + chips - back * (1 - 2 * core), chips), chips)
             columns = pl.ds(pl.multiple_of(home * (2 * members), 2 * members), 2 * members)
-            copy = pltpu.make_async_copy(source, out.at[some, :, columns], sem)
+            copy = pltpu.make_async_copy(source, out.at[some, :, columns], sems.at[len(copies)])
             copy.start()
             copies.append(copy)
 
-        for g, (back, _, _) in enumerate(old_groups):
-            send(old_tile.at[g], back, slice(None), sems.at[g, PARTS])
+        for (old_groups, _), old_tile in zip(old, old_refs):
+            for g, (back, _, _) in enumerate(old_groups):
+                send(old_tile.at[g], back, slice(None))
         for g in range(count):
             for side, piece in ((core, pieces[2 * g]), (1 - core, pieces[2 * g + 1])):
                 rows = pl.ds(pl.multiple_of((2 * g + side) * members, members), members)
@@ -161,7 +162,7 @@
             for g, (back, _, _) in enumerate(groups):
                 tile[g, some] = sums[:, :, 2 * g * members : 2 * (g + 1) * members]
                 if end:
-                    send(tile.at[g, some], back, some, sems.at[g, part])
+                    send(tile.at[g, some], back, some)
         for copy in copies:
             copy.wait()
 
@@ -169,19 +170,19 @@
     anywhere = pl.BlockSpec(memory_space=pl.ANY)
     tile_shape = (count, shape[0], members, 2 * members)
     outs = [] if end else [(pltpu.VMEM(tile_shape, jnp.float32), vmem)]
-    if old_groups:
+    if old or end:
         outs.append((jax.ShapeDtypeStruct(shape, jnp.float32), anywhere))
     scratch = [
         pltpu.VMEM((count * 2 * members, modulated.shape[1]), jnp.bfloat16),
-        pltpu.SemaphoreType.DMA((max(count, len(old_groups)), PARTS + 1)),
+        pltpu.SemaphoreType.DMA((max(1, sum(len(old_groups) for old_groups, _ in old) + count * PARTS),)),
     ]
     got = pl.pallas_call(
         body,
         out_shape=[shaped for shaped, _ in outs],
-        in_specs=[vmem] * (1 + len(flat)) + [vmem] * (old_tiles is not None) + [anywhere] * (onto is not None),
+        in_specs=[vmem] * first_onto + [anywhere] * (onto is not None),
         out_specs=[spec for _, spec in outs],
         scratch_shapes=scratch + ([pltpu.VMEM(tile_shape, jnp.float32)] if end else []),
-        input_output_aliases={} if onto is None else {2 + len(flat): len(outs) - 1},
+        input_output_aliases={} if onto is None else {first_onto: len(outs) - 1},
         compiler_params=pltpu.CompilerParams(vmem_limit_bytes=ROOM),
         cost_estimate=pl.CostEstimate(
             flops=4 * count * members * modulated.size, bytes_accessed=0, transcendentals=0
@@ -190,12 +191,10 @@
     )(
         near(modulated),
         *[near(piece) for piece in flat],
-        *([] if old_tiles is None else [near(old_tiles)]),
+        *[near(tiles) for tiles in old_tiles],
         *([] if onto is None else [onto]),
     )
-    if end:
-        return got[0]
-    return groups, got[0], got[1] if old_groups else None
+    return got[0] if len(got) == 1 else got
 
 
 def per_device(spectra, gap_mask):
@@ -216,14 +215,15 @@
     def swap(array):
         return lax.ppermute(array, "blk", [(i, i ^ 1) for i in range(devices)])
 
-    def add(groups, before, end=False):
-        return correlate(modulated, groups, chips, shape, before, end)
+    def add(groups, **how):
+        return correlate(modulated, groups, chips, shape, **how)
 
     white, tables = whiten(spectra, gap_mask)
     modulated = modulate(white, tables)
 
     mine, other = white, swap(white)
-    out = add([(0, mine, other)], None)
+    groups = [(0, mine, other)]
+    kept = [(groups, add(groups))]
     final = chips // 2
     for step in range(1, final):
         mine = onward(mine, step)
@@ -233,10 +233,14 @@
             groups = [(-step, other, mine), (step, mine_there, other_there)]
         else:
             groups = [(step, mine, other), (-step, other_there, mine_there)]
-        out = add(groups, out)
+        if step + 1 < final:
+            kept.append((groups, add(groups)))
+    tiles, out = add(groups[:1], old=kept)
+    tiles, out = add(groups[1:], old=[(groups[:1], tiles)], onto=out)
     last = onward(mine, final)
     there = swap(last)
-    return add([(final, there, last) if final % 2 else (final, last, there)], out, end=True)
+    ends = [(final, there, last) if final % 2 else (final, last, there)]
+    return add(ends, old=[(groups[1:], tiles)], onto=out, end=True)
 
 
 def solution(mesh):

time: 30.6 us -> 30.8 us (level)
    pallas_call x5 -> x6, Pallas kernels: 5.87 us -> 6.05 us  [correlate(): pl.pallas_call(body, out_shape=[shaped for shaped, _ in outs], in_specs=[...]
  transfers between devices with their start and end apart: 15 -> 15, of which waited for: 5 -> 5; matrix products, arithmetic and copies ran while one was open for 0% -> 0% of each run, Pallas kernels for 16% -> 17%
where the time goes in v3:
time: 30.8 us; the launch traced here: 30.7 us
  starting transfers between devices  15 us (49%)
  waiting for transfers between devices  7.83 us (25%)
  Pallas kernels  7.73 us (25%)
    ppermute x7, starting transfers between devices, onward(): return lax.ppermute(array, 'blk', pairs)  12.8 us
    ppermute x7, waiting for transfers between devices, onward(): return lax.ppermute(array, 'blk', pairs)  7.81 us
    pallas_call x6, Pallas kernels, correlate(): pl.pallas_call(body, out_shape=[shaped for shaped, _ in outs], in_specs=[...  6.05 us
    ppermute x8, starting transfers between devices, swap(): return lax.ppermute(array, 'blk', [(i, i ^ 1) for i in range(devices)])  2.2 us
    pallas_call x1, Pallas kernels, whiten(): pl.pallas_call(whiten_body, out_shape=[pltpu.VMEM((members, 2 * wide), jn...  1.29 us
  transfers between devices with their start and end apart: 15, of which 5 were waited for; matrix products, arithmetic and copies ran while one was open for 0% of the time, Pallas kernels for 17%

profile of v3, /device:TPU:0, one launch (start us, length us, event | category | flops | bytes accessed | tf_op | source)
XLA Modules:
  0.0 30.7 jit_solution(8433876126463406073)
XLA Ops:
  0.0 1.3 %whiten.1 = (bf16[64,1536]{1,0:T(8,128)(2,1)S(1)}, f32[16,768]{1,0:T(8,128)S(1)}) custom-call(bf16[2,64,768]{2,1,0:T(8,128)(2,1)} %spectra.1, s32[48,64]{1,0:T(8,128)} %bitcast.1, f32[16,768]{1,0:T(8,128)} %constant.2.clone.tables), custom_call_target="tpu_custom_call" | custom-call | tf_op jit(solution)/shard_map/whiten/pallas_call | solution.py:72
  1.3 0.6 %collective-permute-start.6 = (bf16[64,1536]{1,0:T(8,128)(2,1)S(1)}, bf16[64,1536]{1,0:T(8,128)(2,1)S(1)}, u32[]{:S(2)}, u32[]{:S(2)}) collective-permute-start(bf16[64,1536]{1,0:T(8,128)(2,1)S(1)} %get-tuple-element.11.white.rest_0_), channel_id=1, source_target_pairs={{0,1},{1,0},{2,3},{3,2},{4,5},{5,4},{6,7},{7,6},{8,9},{9,8},{10,11... | collective-permute-start | bytes 589832 | tf_op jit(solution)/shard_map/ppermute | solution.py:216
  1.9 2.7 %collective-permute-start = (bf16[64,1536]{1,0:T(8,128)(2,1)S(1)}, bf16[64,1536]{1,0:T(8,128)(2,1)S(1)}, u32[]{:S(2)}, u32[]{:S(2)}) collective-permute-start(bf16[64,1536]{1,0:T(8,128)(2,1)S(1)} %get-tuple-element.11.white.rest_0_), channel_id=1, source_target_pairs={{0,5},{1,2},{4,9},{5,0},{8,13},{9,4},{12,15},{13,8},{14,11},{15,12... | collective-permute-start | bytes 589832 | tf_op jit(solution)/shard_map/ppermute | solution.py:213
  4.5 1.1 %collective-permute-start.7 = (bf16[64,1536]{1,0:T(8,128)(2,1)S(1)}, bf16[64,1536]{1,0:T(8,128)(2,1)S(1)}, u32[]{:S(2)}, u32[]{:S(2)}) collective-permute-start(bf16[64,1536]{1,0:T(8,128)(2,1)S(1)} %collective-permute-done.6.rest_1_), channel_id=1, source_target_pairs={{0,5},{1,2},{4,9},{5,0},{8,13},{9,4},{12,15},{13,8},{14,11},{15,12... | collective-permute-start | bytes 589832 | tf_op jit(solution)/shard_map/ppermute | solution.py:213
  5.6 2.3 %collective-permute-done.rest_1_ = bf16[64,1536]{1,0:T(8,128)(2,1)S(1)} collective-permute-done((bf16[64,1536]{1,0:T(8,128)(2,1)S(1)}, bf16[64,1536]{1,0:T(8,128)(2,1)S(1)}, u32[]{:S(2)}, u32[]{:S(2)}) %collective-permute-start) | collective-permute-done | bytes 196640 | tf_op jit(solution)/shard_map/ppermute | solution.py:213
  7.9 2.0 %collective-permute-start.1 = (bf16[64,1536]{1,0:T(8,128)(2,1)S(1)}, bf16[64,1536]{1,0:T(8,128)(2,1)S(1)}, u32[]{:S(2)}, u32[]{:S(2)}) collective-permute-start(bf16[64,1536]{1,0:T(8,128)(2,1)S(1)} %collective-permute-done.rest_1_), channel_id=1, source_target_pairs={{1,4},{0,3},{5,8},{4,1},{9,12},{8,5},{13,14},{12,9},{15,10},{14,13... | collective-permute-start | bytes 589832 | tf_op jit(solution)/shard_map/ppermute | solution.py:213
  9.9 0.1 collective-permute-done.7.rest_0_
  10.0 1.7 %collective-permute-start.8 = (bf16[64,1536]{1,0:T(8,128)(2,1)S(1)}, bf16[64,1536]{1,0:T(8,128)(2,1)S(1)}, u32[]{:S(2)}, u32[]{:S(2)}) collective-permute-start(bf16[64,1536]{1,0:T(8,128)(2,1)S(1)} %collective-permute-done.7.rest_0_), channel_id=1, source_target_pairs={{1,4},{0,3},{5,8},{4,1},{9,12},{8,5},{13,14},{12,9},{15,10},{14,13... | collective-permute-start | bytes 589832 | tf_op jit(solution)/shard_map/ppermute | solution.py:213
  11.7 1.5 %collective-permute-done.1.rest_0_ = bf16[64,1536]{1,0:T(8,128)(2,1)S(1)} collective-permute-done((bf16[64,1536]{1,0:T(8,128)(2,1)S(1)}, bf16[64,1536]{1,0:T(8,128)(2,1)S(1)}, u32[]{:S(2)}, u32[]{:S(2)}) %collective-permute-start.1) | collective-permute-done | bytes 196640 | tf_op jit(solution)/shard_map/ppermute | solution.py:213
  13.2 2.1 %collective-permute-start.2 = (bf16[64,1536]{1,0:T(8,128)(2,1)S(1)}, bf16[64,1536]{1,0:T(8,128)(2,1)S(1)}, u32[]{:S(2)}, u32[]{:S(2)}) collective-permute-start(bf16[64,1536]{1,0:T(8,128)(2,1)S(1)} %collective-permute-done.1.rest_0_), channel_id=1, source_target_pairs={{0,5},{1,2},{4,9},{5,0},{8,13},{9,4},{12,15},{13,8},{14,11},{15,12... | collective-permute-start | bytes 589832 | tf_op jit(solution)/shard_map/ppermute | solution.py:213
  15.3 0.5 %collective-permute-start.12 = (bf16[64,1536]{1,0:T(8,128)(2,1)S(1)}, bf16[64,1536]{1,0:T(8,128)(2,1)S(1)}, u32[]{:S(2)}, u32[]{:S(2)}) collective-permute-start(bf16[64,1536]{1,0:T(8,128)(2,1)S(1)} %collective-permute-done.7.rest_0_), channel_id=1, source_target_pairs={{0,1},{1,0},{2,3},{3,2},{4,5},{5,4},{6,7},{7,6},{8,9},{9,8},{10,11... | collective-permute-start | bytes 589832 | tf_op jit(solution)/shard_map/ppermute | solution.py:216
  15.8 1.3 %collective-permute-start.9 = (bf16[64,1536]{1,0:T(8,128)(2,1)S(1)}, bf16[64,1536]{1,0:T(8,128)(2,1)S(1)}, u32[]{:S(2)}, u32[]{:S(2)}) collective-permute-start(bf16[64,1536]{1,0:T(8,128)(2,1)S(1)} %collective-permute-done.8.rest_1_), channel_id=1, source_target_pairs={{0,5},{1,2},{4,9},{5,0},{8,13},{9,4},{12,15},{13,8},{14,11},{15,12... | collective-permute-start | bytes 589832 | tf_op jit(solution)/shard_map/ppermute | solution.py:213
  17.1 1.5 %collective-permute-done.2.rest_1_ = bf16[64,1536]{1,0:T(8,128)(2,1)S(1)} collective-permute-done((bf16[64,1536]{1,0:T(8,128)(2,1)S(1)}, bf16[64,1536]{1,0:T(8,128)(2,1)S(1)}, u32[]{:S(2)}, u32[]{:S(2)}) %collective-permute-start.2) | collective-permute-done | bytes 196640 | tf_op jit(solution)/shard_map/ppermute | solution.py:213
  18.7 2.0 %collective-permute-start.3 = (bf16[64,1536]{1,0:T(8,128)(2,1)S(1)}, bf16[64,1536]{1,0:T(8,128)(2,1)S(1)}, u32[]{:S(2)}, u32[]{:S(2)}) collective-permute-start(bf16[64,1536]{1,0:T(8,128)(2,1)S(1)} %collective-permute-done.2.rest_1_), channel_id=1, source_target_pairs={{1,4},{0,3},{5,8},{4,1},{9,12},{8,5},{13,14},{12,9},{15,10},{14,13... | collective-permute-start | bytes 589832 | tf_op jit(solution)/shard_map/ppermute | solution.py:213
  20.7 0.5 %collective-permute-start.13 = (bf16[64,1536]{1,0:T(8,128)(2,1)S(1)}, bf16[64,1536]{1,0:T(8,128)(2,1)S(1)}, u32[]{:S(2)}, u32[]{:S(2)}) collective-permute-start(bf16[64,1536]{1,0:T(8,128)(2,1)S(1)} %collective-permute-done.8.rest_1_), channel_id=1, source_target_pairs={{0,1},{1,0},{2,3},{3,2},{4,5},{5,4},{6,7},{7,6},{8,9},{9,8},{10,11... | collective-permute-start | bytes 589832 | tf_op jit(solution)/shard_map/ppermute | solution.py:216
  21.2 0.4 %collective-permute-start.10 = (bf16[64,1536]{1,0:T(8,128)(2,1)S(1)}, bf16[64,1536]{1,0:T(8,128)(2,1)S(1)}, u32[]{:S(2)}, u32[]{:S(2)}) collective-permute-start(bf16[64,1536]{1,0:T(8,128)(2,1)S(1)} %collective-permute-done.9.rest_0_), channel_id=1, source_target_pairs={{0,1},{1,0},{2,3},{3,2},{4,5},{5,4},{6,7},{7,6},{8,9},{9,8},{10,11... | collective-permute-start | bytes 589832 | tf_op jit(solution)/shard_map/ppermute | solution.py:216
  21.7 2.3 %collective-permute-done.3.rest_0_ = bf16[64,1536]{1,0:T(8,128)(2,1)S(1)} collective-permute-done((bf16[64,1536]{1,0:T(8,128)(2,1)S(1)}, bf16[64,1536]{1,0:T(8,128)(2,1)S(1)}, u32[]{:S(2)}, u32[]{:S(2)}) %collective-permute-start.3) | collective-permute-done | bytes 196640 | tf_op jit(solution)/shard_map/ppermute | solution.py:213
  24.1 0.4 %modulate.1.modulated = bf16[512,1536]{1,0:T(8,128)(2,1)S(1)} custom-call(bf16[64,1536]{1,0:T(8,128)(2,1)S(1)} %get-tuple-element.11.white.rest_0_, f32[16,768]{1,0:T(8,128)S(1)} %get-tuple-element.12.tables), custom_call_target="tpu_custom_call" | custom-call | flops 9437184 | tf_op jit(solution)/shard_map/modulate/pallas_call | solution.py:99
  24.5 0.6 %correlate.6.rest_2_ = f32[1,8,64,128]{3,2,1,0:T(8,128)S(1)} custom-call(bf16[512,1536]{1,0:T(8,128)(2,1)S(1)} %modulate.1.modulated, bf16[64,1536]{1,0:T(8,128)(2,1)S(1)} %get-tuple-element.11.white.rest_0_, bf16[64,1536]{1,0:T(8,128)(2,1)S(1)} %collective-permute-done.6.rest_1_), custom_call_target="tpu_custom_call" | custom-call | flops 201326592 | tf_op jit(solution)/shard_map/correlate/pallas_call | solution.py:179
  25.1 0.7 %correlate.7.rest_3_ = f32[2,8,64,128]{3,2,1,0:T(8,128)S(1)} custom-call(bf16[512,1536]{1,0:T(8,128)(2,1)S(1)} %modulate.1.modulated, bf16[64,1536]{1,0:T(8,128)(2,1)S(1)} %collective-permute-done.7.rest_0_, bf16[64,1536]{1,0:T(8,128)(2,1)S(1)} %collective-permute-done.rest_1_, bf16[64,1536]{1,0:T(8,128)(2,1)S(1)} %collective-permute-done.11.rest_2_, ...), custom_call_target="tpu_custom_call" | custom-call | flops 402653184 | tf_op jit(solution)/shard_map/correlate/pallas_call | solution.py:179
  25.8 0.7 %correlate.8.rest_4_ = f32[2,8,64,128]{3,2,1,0:T(8,128)S(1)} custom-call(bf16[512,1536]{1,0:T(8,128)(2,1)S(1)} %modulate.1.modulated, bf16[64,1536]{1,0:T(8,128)(2,1)S(1)} %collective-permute-done.1.rest_0_, bf16[64,1536]{1,0:T(8,128)(2,1)S(1)} %collective-permute-done.8.rest_1_, bf16[64,1536]{1,0:T(8,128)(2,1)S(1)} %collective-permute-done.13.rest_2_, ...), custom_call_target="tpu_custom_call" | custom-call | flops 402653184 | tf_op jit(solution)/shard_map/correlate/pallas_call | solution.py:179
  26.5 1.6 %correlate.9 = (f32[1,8,64,128]{3,2,1,0:T(8,128)S(1)}, f32[8,64,1024]{2,1,0:T(8,128)}) custom-call(bf16[512,1536]{1,0:T(8,128)(2,1)S(1)} %modulate.1.modulated, bf16[64,1536]{1,0:T(8,128)(2,1)S(1)} %collective-permute-done.9.rest_0_, bf16[64,1536]{1,0:T(8,128)(2,1)S(1)} %collective-permute-done.2.rest_1_, f32[1,8,64,128]{3,2,1,0:T(8,128)S(1)} %correlate.6.rest_2_, ...), custom_call_target="tpu_custom_call" | custom-call | flops 201326592 | tf_op jit(solution)/shard_map/correlate/pallas_call | solution.py:179
  28.1 1.2 %correlate.10 = (f32[1,8,64,128]{3,2,1,0:T(8,128)S(1)}, f32[8,64,1024]{2,1,0:T(8,128)}) custom-call(bf16[512,1536]{1,0:T(8,128)(2,1)S(1)} %modulate.1.modulated, bf16[64,1536]{1,0:T(8,128)(2,1)S(1)} %collective-permute-done.5.rest_0_, bf16[64,1536]{1,0:T(8,128)(2,1)S(1)} %collective-permute-done.10.rest_1_, ...), custom_call_target="tpu_custom_call", output_to_operand_aliasing={{1}: (4, {})} | custom-call | flops 201326592 | tf_op jit(solution)/shard_map/correlate/pallas_call | solution.py:179
  29.3 1.3 %correlate.11 = f32[8,64,1024]{2,1,0:T(8,128)} custom-call(bf16[512,1536]{1,0:T(8,128)(2,1)S(1)} %modulate.1.modulated, bf16[64,1536]{1,0:T(8,128)(2,1)S(1)} %collective-permute-done.3.rest_0_, bf16[64,1536]{1,0:T(8,128)(2,1)S(1)} %collective-permute-done.4.rest_1_, f32[1,8,64,128]{3,2,1,0:T(8,128)S(1)} %get-tuple-element.15.rest_2_, ...), custom_call_target="tpu_custom_call", output_to_operand_aliasing={{}: (4, {})} | custom-call | flops 201326592 | tf_op jit(solution)/shard_map/correlate/pallas_call | solution.py:179
  (14 shorter events, 0.2 us)
Async XLA Ops:
  1.3 3.2 %collective-permute-start.6 = (bf16[64,1536]{1,0:T(8,128)(2,1)S(1)}, bf16[64,1536]{1,0:T(8,128)(2,1)S(1)}, u32[]{:S(2)}, u32[]{:S(2)}) collective-permute-start(bf16[64,1536]{1,0:T(8,128)(2,1)S(1)} %get-tuple-element.11.white.rest_0_), channel_id=1, source_target_pairs={{0,1},{1,0},{2,3},{3,2},{4,5},{5,4},{6,7},{7,6},{8,9},{9,8},{10,11... | collective-permute-start | bytes 589832 | tf_op jit(solution)/shard_map/ppermute | solution.py:216
  1.9 6.0 %collective-permute-start = (bf16[64,1536]{1,0:T(8,128)(2,1)S(1)}, bf16[64,1536]{1,0:T(8,128)(2,1)S(1)}, u32[]{:S(2)}, u32[]{:S(2)}) collective-permute-start(bf16[64,1536]{1,0:T(8,128)(2,1)S(1)} %get-tuple-element.11.white.rest_0_), channel_id=1, source_target_pairs={{0,5},{1,2},{4,9},{5,0},{8,13},{9,4},{12,15},{13,8},{14,11},{15,12... | collective-permute-start | bytes 589832 | tf_op jit(solution)/shard_map/ppermute | solution.py:213
  4.5 5.5 %collective-permute-start.7 = (bf16[64,1536]{1,0:T(8,128)(2,1)S(1)}, bf16[64,1536]{1,0:T(8,128)(2,1)S(1)}, u32[]{:S(2)}, u32[]{:S(2)}) collective-permute-start(bf16[64,1536]{1,0:T(8,128)(2,1)S(1)} %collective-permute-done.6.rest_1_), channel_id=1, source_target_pairs={{0,5},{1,2},{4,9},{5,0},{8,13},{9,4},{12,15},{13,8},{14,11},{15,12... | collective-permute-start | bytes 589832 | tf_op jit(solution)/shard_map/ppermute | solution.py:213
  7.9 5.3 %collective-permute-start.1 = (bf16[64,1536]{1,0:T(8,128)(2,1)S(1)}, bf16[64,1536]{1,0:T(8,128)(2,1)S(1)}, u32[]{:S(2)}, u32[]{:S(2)}) collective-permute-start(bf16[64,1536]{1,0:T(8,128)(2,1)S(1)} %collective-permute-done.rest_1_), channel_id=1, source_target_pairs={{1,4},{0,3},{5,8},{4,1},{9,12},{8,5},{13,14},{12,9},{15,10},{14,13... | collective-permute-start | bytes 589832 | tf_op jit(solution)/shard_map/ppermute | solution.py:213
  10.0 5.8 %collective-permute-start.8 = (bf16[64,1536]{1,0:T(8,128)(2,1)S(1)}, bf16[64,1536]{1,0:T(8,128)(2,1)S(1)}, u32[]{:S(2)}, u32[]{:S(2)}) collective-permute-start(bf16[64,1536]{1,0:T(8,128)(2,1)S(1)} %collective-permute-done.7.rest_0_), channel_id=1, source_target_pairs={{1,4},{0,3},{5,8},{4,1},{9,12},{8,5},{13,14},{12,9},{15,10},{14,13... | collective-permute-start | bytes 589832 | tf_op jit(solution)/shard_map/ppermute | solution.py:213
  13.2 5.4 %collective-permute-start.2 = (bf16[64,1536]{1,0:T(8,128)(2,1)S(1)}, bf16[64,1536]{1,0:T(8,128)(2,1)S(1)}, u32[]{:S(2)}, u32[]{:S(2)}) collective-permute-start(bf16[64,1536]{1,0:T(8,128)(2,1)S(1)} %collective-permute-done.1.rest_0_), channel_id=1, source_target_pairs={{0,5},{1,2},{4,9},{5,0},{8,13},{9,4},{12,15},{13,8},{14,11},{15,12... | collective-permute-start | bytes 589832 | tf_op jit(solution)/shard_map/ppermute | solution.py:213
  15.3 5.3 %collective-permute-start.11 = (bf16[64,1536]{1,0:T(8,128)(2,1)S(1)}, bf16[64,1536]{1,0:T(8,128)(2,1)S(1)}, u32[]{:S(2)}, u32[]{:S(2)}) collective-permute-start(bf16[64,1536]{1,0:T(8,128)(2,1)S(1)} %collective-permute-done.rest_1_), channel_id=1, source_target_pairs={{0,1},{1,0},{2,3},{3,2},{4,5},{5,4},{6,7},{7,6},{8,9},{9,8},{10,11... | collective-permute-start | bytes 589832 | tf_op jit(solution)/shard_map/ppermute | solution.py:216
  15.3 5.8 %collective-permute-start.12 = (bf16[64,1536]{1,0:T(8,128)(2,1)S(1)}, bf16[64,1536]{1,0:T(8,128)(2,1)S(1)}, u32[]{:S(2)}, u32[]{:S(2)}) collective-permute-start(bf16[64,1536]{1,0:T(8,128)(2,1)S(1)} %collective-permute-done.7.rest_0_), channel_id=1, source_target_pairs={{0,1},{1,0},{2,3},{3,2},{4,5},{5,4},{6,7},{7,6},{8,9},{9,8},{10,11... | collective-permute-start | bytes 589832 | tf_op jit(solution)/shard_map/ppermute | solution.py:216
  15.8 5.4 %collective-permute-start.9 = (bf16[64,1536]{1,0:T(8,128)(2,1)S(1)}, bf16[64,1536]{1,0:T(8,128)(2,1)S(1)}, u32[]{:S(2)}, u32[]{:S(2)}) collective-permute-start(bf16[64,1536]{1,0:T(8,128)(2,1)S(1)} %collective-permute-done.8.rest_1_), channel_id=1, source_target_pairs={{0,5},{1,2},{4,9},{5,0},{8,13},{9,4},{12,15},{13,8},{14,11},{15,12... | collective-permute-start | bytes 589832 | tf_op jit(solution)/shard_map/ppermute | solution.py:213
  18.7 5.3 %collective-permute-start.3 = (bf16[64,1536]{1,0:T(8,128)(2,1)S(1)}, bf16[64,1536]{1,0:T(8,128)(2,1)S(1)}, u32[]{:S(2)}, u32[]{:S(2)}) collective-permute-start(bf16[64,1536]{1,0:T(8,128)(2,1)S(1)} %collective-permute-done.2.rest_1_), channel_id=1, source_target_pairs={{1,4},{0,3},{5,8},{4,1},{9,12},{8,5},{13,14},{12,9},{15,10},{14,13... | collective-permute-start | bytes 589832 | tf_op jit(solution)/shard_map/ppermute | solution.py:213
  20.6 5.2 %collective-permute-start.14 = (bf16[64,1536]{1,0:T(8,128)(2,1)S(1)}, bf16[64,1536]{1,0:T(8,128)(2,1)S(1)}, u32[]{:S(2)}, u32[]{:S(2)}) collective-permute-start(bf16[64,1536]{1,0:T(8,128)(2,1)S(1)} %collective-permute-done.1.rest_0_), channel_id=1, source_target_pairs={{0,1},{1,0},{2,3},{3,2},{4,5},{5,4},{6,7},{7,6},{8,9},{9,8},{10,11... | collective-permute-start | bytes 589832 | tf_op jit(solution)/shard_map/ppermute | solution.py:216
  20.7 5.2 %collective-permute-start.13 = (bf16[64,1536]{1,0:T(8,128)(2,1)S(1)}, bf16[64,1536]{1,0:T(8,128)(2,1)S(1)}, u32[]{:S(2)}, u32[]{:S(2)}) collective-permute-start(bf16[64,1536]{1,0:T(8,128)(2,1)S(1)} %collective-permute-done.8.rest_1_), channel_id=1, source_target_pairs={{0,1},{1,0},{2,3},{3,2},{4,5},{5,4},{6,7},{7,6},{8,9},{9,8},{10,11... | collective-permute-start | bytes 589832 | tf_op jit(solution)/shard_map/ppermute | solution.py:216
  21.2 6.9 %collective-permute-start.5 = (bf16[64,1536]{1,0:T(8,128)(2,1)S(1)}, bf16[64,1536]{1,0:T(8,128)(2,1)S(1)}, u32[]{:S(2)}, u32[]{:S(2)}) collective-permute-start(bf16[64,1536]{1,0:T(8,128)(2,1)S(1)} %collective-permute-done.2.rest_1_), channel_id=1, source_target_pairs={{0,1},{1,0},{2,3},{3,2},{4,5},{5,4},{6,7},{7,6},{8,9},{9,8},{10,11... | collective-permute-start | bytes 589832 | tf_op jit(solution)/shard_map/ppermute | solution.py:216
  21.2 6.9 %collective-permute-start.10 = (bf16[64,1536]{1,0:T(8,128)(2,1)S(1)}, bf16[64,1536]{1,0:T(8,128)(2,1)S(1)}, u32[]{:S(2)}, u32[]{:S(2)}) collective-permute-start(bf16[64,1536]{1,0:T(8,128)(2,1)S(1)} %collective-permute-done.9.rest_0_), channel_id=1, source_target_pairs={{0,1},{1,0},{2,3},{3,2},{4,5},{5,4},{6,7},{7,6},{8,9},{9,8},{10,11... | collective-permute-start | bytes 589832 | tf_op jit(solution)/shard_map/ppermute | solution.py:216
  24.0 5.3 %collective-permute-start.4 = (bf16[64,1536]{1,0:T(8,128)(2,1)S(1)}, bf16[64,1536]{1,0:T(8,128)(2,1)S(1)}, u32[]{:S(2)}, u32[]{:S(2)}) collective-permute-start(bf16[64,1536]{1,0:T(8,128)(2,1)S(1)} %collective-permute-done.3.rest_0_), channel_id=1, source_target_pairs={{0,1},{1,0},{2,3},{3,2},{4,5},{5,4},{6,7},{7,6},{8,9},{9,8},{10,11... | collective-permute-start | bytes 589832 | tf_op jit(solution)/shard_map/ppermute | solution.py:216

commit v4 on v2

--- a/solution.py
+++ b/solution.py
@@ -35,45 +35,68 @@
     return pltpu.with_memory_space_constraint(array, pltpu.HBM)
 
 
-def whiten_body(spectra, gap_mask, tables, out, tables_near):
-    tables_near[...] = tables[...]
+def whiten_body(spectra_far, gap_mask_far, tables_far, out, tables, spectra, gap_mask, sems):
+    copies = [
+        pltpu.make_async_copy(source, target, sems.at[i])
+        for i, (source, target) in enumerate(
+            ((gap_mask_far, gap_mask), (spectra_far, spectra), (tables_far, tables))
+        )
+    ]
+    for copy in copies:
+        copy.start()
     wide = spectra.shape[2]
     bin_count = wide // gap_mask.shape[0]
+    lane = lax.broadcasted_iota(jnp.int32, (8, wide), 1) % bin_count
+    count = jnp.ones(lane.shape, jnp.float32)
+    keeps = []
+    for step in range(1, REACH + 1):
+        for keep, by in ((lane + step < bin_count, wide - step), (lane >= step, step)):
+            keeps.append((keep.astype(jnp.float32), by))
+            count = count + keeps[-1][0]
+    share = 1.0 / count
+    window = lax.broadcasted_iota(jnp.int32, (gap_mask.shape[0], wide), 1) // bin_count
+    spread = window == lax.broadcasted_iota(jnp.int32, window.shape, 0)
+    spread = spread.astype(jnp.float32).astype(jnp.bfloat16)
+    copies[0].wait()
+    kept = lax.dot_general(
+        gap_mask[...].astype(jnp.float32).astype(jnp.bfloat16),
+        spread,
+        (((0,), (0,)), ((), ())),
+        preferred_element_type=jnp.float32,
+    )
+    copies[1].wait()
     real = spectra[0].astype(jnp.float32)
     imag = spectra[1].astype(jnp.float32)
     amplitude = jnp.sqrt(real * real + imag * imag)
-    lane = lax.broadcasted_iota(jnp.int32, amplitude.shape, 1) % bin_count
+    rows = (amplitude.shape[0] // 8, 1)
     total = amplitude
-    count = jnp.ones(amplitude.shape, jnp.float32)
-    for step in range(1, REACH + 1):
-        above = lane + step < bin_count
-        below = lane >= step
-        total = total + jnp.where(above, pltpu.roll(amplitude, wide - step, 1), 0.0)
-        total = total + jnp.where(below, pltpu.roll(amplitude, step, 1), 0.0)
-        count = count + above.astype(jnp.float32) + below.astype(jnp.float32)
-    level = jnp.maximum(total / count, level_floor)
-    window = lax.broadcasted_iota(jnp.int32, (gap_mask.shape[0], wide), 1) // bin_count
-    spread = window == lax.broadcasted_iota(jnp.int32, window.shape, 0)
-    kept = lax.dot_general(
-        gap_mask[...].astype(jnp.float32).astype(jnp.bfloat16),
-        spread.astype(jnp.float32).astype(jnp.bfloat16),
-        (((0,), (0,)), ((), ())),
-        preferred_element_type=jnp.float32,
-    )
+    for keep, by in keeps:
+        total = total + jnp.tile(keep, rows) * pltpu.roll(amplitude, by, 1)
+    level = jnp.maximum(total * jnp.tile(share, rows), level_floor)
     factor = kept / level
     out[:, :wide] = (real * factor).astype(jnp.bfloat16)
     out[:, wide:] = (imag * factor).astype(jnp.bfloat16)
+    copies[2].wait()
 
 
 def whiten(spectra, gap_mask):
     members, wide = spectra.shape[1:]
     win_count = gap_mask.shape[1]
     tables = phase_tables(wide // win_count, win_count, LAGS)
+    vmem = pl.BlockSpec(memory_space=pltpu.VMEM)
+    anywhere = pl.BlockSpec(memory_space=pl.ANY)
     return pl.pallas_call(
         whiten_body,
         out_shape=[
             pltpu.VMEM((members, 2 * wide), jnp.bfloat16),
             pltpu.VMEM(tables.shape, jnp.float32),
+        ],
+        in_specs=[anywhere] * 3,
+        out_specs=[vmem] * 2,
+        scratch_shapes=[
+            pltpu.VMEM(spectra.shape, spectra.dtype),
+            pltpu.VMEM((win_count, members), gap_mask.dtype),
+            pltpu.SemaphoreType.DMA((3,)),
         ],
         compiler_params=pltpu.CompilerParams(vmem_limit_bytes=ROOM),
         name="whiten",

time: 30.6 us -> 30.6 us (level)
  no operation moved by 1% of the time
where the time goes in v4:
time: 30.6 us; the launch traced here: 30.5 us
  starting transfers between devices  15 us (49%)
  waiting for transfers between devices  7.83 us (26%)
  Pallas kernels  7.57 us (25%)
    ppermute x7, starting transfers between devices, onward(): return lax.ppermute(array, 'blk', pairs)  12.8 us
    ppermute x7, waiting for transfers between devices, onward(): return lax.ppermute(array, 'blk', pairs)  7.81 us
    pallas_call x5, Pallas kernels, correlate(): pl.pallas_call(body, out_shape=[shaped for shaped, _ in outs], in_specs=[...  5.87 us
    ppermute x8, starting transfers between devices, swap(): return lax.ppermute(array, 'blk', [(i, i ^ 1) for i in range(devices)])  2.2 us
    pallas_call x1, Pallas kernels, whiten(): pl.pallas_call(whiten_body, out_shape=[pltpu.VMEM((members, 2 * wide), jn...  1.31 us
  transfers between devices with their start and end apart: 15, of which 5 were waited for; matrix products, arithmetic and copies ran while one was open for 0% of the time, Pallas kernels for 16%

profile of v4, /device:TPU:0, one launch (start us, length us, event | category | flops | bytes accessed | tf_op | source)
XLA Modules:
  0.0 30.5 jit_solution(18374369384356674009)
XLA Ops:
  0.0 1.3 %whiten.1 = (bf16[64,1536]{1,0:T(8,128)(2,1)S(1)}, f32[16,768]{1,0:T(8,128)S(1)}) custom-call(bf16[2,64,768]{2,1,0:T(8,128)(2,1)} %spectra_far.1, s32[48,64]{1,0:T(8,128)} %bitcast.1, f32[16,768]{1,0:T(8,128)} %constant.2.clone.tables_far), custom_call_target="tpu_custom_call" | custom-call | tf_op jit(solution)/shard_map/whiten/pallas_call | solution.py:88
  1.3 0.6 %collective-permute-start.5 = (bf16[64,1536]{1,0:T(8,128)(2,1)S(1)}, bf16[64,1536]{1,0:T(8,128)(2,1)S(1)}, u32[]{:S(2)}, u32[]{:S(2)}) collective-permute-start(bf16[64,1536]{1,0:T(8,128)(2,1)S(1)} %get-tuple-element.13.white.rest_0_), channel_id=1, source_target_pairs={{0,1},{1,0},{2,3},{3,2},{4,5},{5,4},{6,7},{7,6},{8,9},{9,8},{10,11... | collective-permute-start | bytes 589832 | tf_op jit(solution)/shard_map/ppermute | solution.py:240
  1.9 2.7 %collective-permute-start = (bf16[64,1536]{1,0:T(8,128)(2,1)S(1)}, bf16[64,1536]{1,0:T(8,128)(2,1)S(1)}, u32[]{:S(2)}, u32[]{:S(2)}) collective-permute-start(bf16[64,1536]{1,0:T(8,128)(2,1)S(1)} %get-tuple-element.13.white.rest_0_), channel_id=1, source_target_pairs={{0,5},{1,2},{4,9},{5,0},{8,13},{9,4},{12,15},{13,8},{14,11},{15,12... | collective-permute-start | bytes 589832 | tf_op jit(solution)/shard_map/ppermute | solution.py:237
  4.6 1.1 %collective-permute-start.6 = (bf16[64,1536]{1,0:T(8,128)(2,1)S(1)}, bf16[64,1536]{1,0:T(8,128)(2,1)S(1)}, u32[]{:S(2)}, u32[]{:S(2)}) collective-permute-start(bf16[64,1536]{1,0:T(8,128)(2,1)S(1)} %collective-permute-done.5.rest_1_), channel_id=1, source_target_pairs={{0,5},{1,2},{4,9},{5,0},{8,13},{9,4},{12,15},{13,8},{14,11},{15,12... | collective-permute-start | bytes 589832 | tf_op jit(solution)/shard_map/ppermute | solution.py:237
  5.6 2.3 %collective-permute-done.rest_1_ = bf16[64,1536]{1,0:T(8,128)(2,1)S(1)} collective-permute-done((bf16[64,1536]{1,0:T(8,128)(2,1)S(1)}, bf16[64,1536]{1,0:T(8,128)(2,1)S(1)}, u32[]{:S(2)}, u32[]{:S(2)}) %collective-permute-start) | collective-permute-done | bytes 196640 | tf_op jit(solution)/shard_map/ppermute | solution.py:237
  7.9 2.0 %collective-permute-start.1 = (bf16[64,1536]{1,0:T(8,128)(2,1)S(1)}, bf16[64,1536]{1,0:T(8,128)(2,1)S(1)}, u32[]{:S(2)}, u32[]{:S(2)}) collective-permute-start(bf16[64,1536]{1,0:T(8,128)(2,1)S(1)} %collective-permute-done.rest_1_), channel_id=1, source_target_pairs={{1,4},{0,3},{5,8},{4,1},{9,12},{8,5},{13,14},{12,9},{15,10},{14,13... | collective-permute-start | bytes 589832 | tf_op jit(solution)/shard_map/ppermute | solution.py:237
  9.9 0.1 collective-permute-done.6.rest_0_
  10.0 1.7 %collective-permute-start.7 = (bf16[64,1536]{1,0:T(8,128)(2,1)S(1)}, bf16[64,1536]{1,0:T(8,128)(2,1)S(1)}, u32[]{:S(2)}, u32[]{:S(2)}) collective-permute-start(bf16[64,1536]{1,0:T(8,128)(2,1)S(1)} %collective-permute-done.6.rest_0_), channel_id=1, source_target_pairs={{1,4},{0,3},{5,8},{4,1},{9,12},{8,5},{13,14},{12,9},{15,10},{14,13... | collective-permute-start | bytes 589832 | tf_op jit(solution)/shard_map/ppermute | solution.py:237
  11.7 1.5 %collective-permute-done.1.rest_0_ = bf16[64,1536]{1,0:T(8,128)(2,1)S(1)} collective-permute-done((bf16[64,1536]{1,0:T(8,128)(2,1)S(1)}, bf16[64,1536]{1,0:T(8,128)(2,1)S(1)}, u32[]{:S(2)}, u32[]{:S(2)}) %collective-permute-start.1) | collective-permute-done | bytes 196640 | tf_op jit(solution)/shard_map/ppermute | solution.py:237
  13.2 2.1 %collective-permute-start.2 = (bf16[64,1536]{1,0:T(8,128)(2,1)S(1)}, bf16[64,1536]{1,0:T(8,128)(2,1)S(1)}, u32[]{:S(2)}, u32[]{:S(2)}) collective-permute-start(bf16[64,1536]{1,0:T(8,128)(2,1)S(1)} %collective-permute-done.1.rest_0_), channel_id=1, source_target_pairs={{0,5},{1,2},{4,9},{5,0},{8,13},{9,4},{12,15},{13,8},{14,11},{15,12... | collective-permute-start | bytes 589832 | tf_op jit(solution)/shard_map/ppermute | solution.py:237
  15.3 0.5 %collective-permute-start.14 = (bf16[64,1536]{1,0:T(8,128)(2,1)S(1)}, bf16[64,1536]{1,0:T(8,128)(2,1)S(1)}, u32[]{:S(2)}, u32[]{:S(2)}) collective-permute-start(bf16[64,1536]{1,0:T(8,128)(2,1)S(1)} %collective-permute-done.6.rest_0_), channel_id=1, source_target_pairs={{0,1},{1,0},{2,3},{3,2},{4,5},{5,4},{6,7},{7,6},{8,9},{9,8},{10,11... | collective-permute-start | bytes 589832 | tf_op jit(solution)/shard_map/ppermute | solution.py:240
  15.8 1.3 %collective-permute-start.8 = (bf16[64,1536]{1,0:T(8,128)(2,1)S(1)}, bf16[64,1536]{1,0:T(8,128)(2,1)S(1)}, u32[]{:S(2)}, u32[]{:S(2)}) collective-permute-start(bf16[64,1536]{1,0:T(8,128)(2,1)S(1)} %collective-permute-done.7.rest_1_), channel_id=1, source_target_pairs={{0,5},{1,2},{4,9},{5,0},{8,13},{9,4},{12,15},{13,8},{14,11},{15,12... | collective-permute-start | bytes 589832 | tf_op jit(solution)/shard_map/ppermute | solution.py:237
  17.1 1.5 %collective-permute-done.2.rest_1_ = bf16[64,1536]{1,0:T(8,128)(2,1)S(1)} collective-permute-done((bf16[64,1536]{1,0:T(8,128)(2,1)S(1)}, bf16[64,1536]{1,0:T(8,128)(2,1)S(1)}, u32[]{:S(2)}, u32[]{:S(2)}) %collective-permute-start.2) | collective-permute-done | bytes 196640 | tf_op jit(solution)/shard_map/ppermute | solution.py:237
  18.7 2.0 %collective-permute-start.3 = (bf16[64,1536]{1,0:T(8,128)(2,1)S(1)}, bf16[64,1536]{1,0:T(8,128)(2,1)S(1)}, u32[]{:S(2)}, u32[]{:S(2)}) collective-permute-start(bf16[64,1536]{1,0:T(8,128)(2,1)S(1)} %collective-permute-done.2.rest_1_), channel_id=1, source_target_pairs={{1,4},{0,3},{5,8},{4,1},{9,12},{8,5},{13,14},{12,9},{15,10},{14,13... | collective-permute-start | bytes 589832 | tf_op jit(solution)/shard_map/ppermute | solution.py:237
  20.7 0.5 %collective-permute-start.11 = (bf16[64,1536]{1,0:T(8,128)(2,1)S(1)}, bf16[64,1536]{1,0:T(8,128)(2,1)S(1)}, u32[]{:S(2)}, u32[]{:S(2)}) collective-permute-start(bf16[64,1536]{1,0:T(8,128)(2,1)S(1)} %collective-permute-done.7.rest_1_), channel_id=1, source_target_pairs={{0,1},{1,0},{2,3},{3,2},{4,5},{5,4},{6,7},{7,6},{8,9},{9,8},{10,11... | collective-permute-start | bytes 589832 | tf_op jit(solution)/shard_map/ppermute | solution.py:240
  21.3 0.4 %collective-permute-start.10 = (bf16[64,1536]{1,0:T(8,128)(2,1)S(1)}, bf16[64,1536]{1,0:T(8,128)(2,1)S(1)}, u32[]{:S(2)}, u32[]{:S(2)}) collective-permute-start(bf16[64,1536]{1,0:T(8,128)(2,1)S(1)} %collective-permute-done.8.rest_0_), channel_id=1, source_target_pairs={{0,1},{1,0},{2,3},{3,2},{4,5},{5,4},{6,7},{7,6},{8,9},{9,8},{10,11... | collective-permute-start | bytes 589832 | tf_op jit(solution)/shard_map/ppermute | solution.py:240
  21.7 2.3 %collective-permute-done.3.rest_0_ = bf16[64,1536]{1,0:T(8,128)(2,1)S(1)} collective-permute-done((bf16[64,1536]{1,0:T(8,128)(2,1)S(1)}, bf16[64,1536]{1,0:T(8,128)(2,1)S(1)}, u32[]{:S(2)}, u32[]{:S(2)}) %collective-permute-start.3) | collective-permute-done | bytes 196640 | tf_op jit(solution)/shard_map/ppermute | solution.py:237
  24.0 0.1 collective-permute-start.4
  24.1 0.4 %modulate.1.modulated = bf16[512,1536]{1,0:T(8,128)(2,1)S(1)} custom-call(bf16[64,1536]{1,0:T(8,128)(2,1)S(1)} %get-tuple-element.13.white.rest_0_, f32[16,768]{1,0:T(8,128)S(1)} %get-tuple-element.14.tables), custom_call_target="tpu_custom_call" | custom-call | flops 9437184 | tf_op jit(solution)/shard_map/modulate/pallas_call | solution.py:122
  24.5 0.6 %correlate.5.rest_4_ = f32[1,8,64,128]{3,2,1,0:T(8,128)S(1)} custom-call(bf16[512,1536]{1,0:T(8,128)(2,1)S(1)} %modulate.1.modulated, bf16[64,1536]{1,0:T(8,128)(2,1)S(1)} %get-tuple-element.13.white.rest_0_, bf16[64,1536]{1,0:T(8,128)(2,1)S(1)} %collective-permute-done.5.rest_1_), custom_call_target="tpu_custom_call" | custom-call | flops 201326592 | tf_op jit(solution)/shard_map/correlate/pallas_call | solution.py:201
  25.2 1.3 %correlate.6 = (f32[2,8,64,128]{3,2,1,0:T(8,128)S(1)}, f32[8,64,1024]{2,1,0:T(8,128)}) custom-call(bf16[512,1536]{1,0:T(8,128)(2,1)S(1)} %modulate.1.modulated, bf16[64,1536]{1,0:T(8,128)(2,1)S(1)} %collective-permute-done.6.rest_0_, bf16[64,1536]{1,0:T(8,128)(2,1)S(1)} %collective-permute-done.rest_1_, ...), custom_call_target="tpu_custom_call" | custom-call | flops 402653184 | tf_op jit(solution)/shard_map/correlate/pallas_call | solution.py:201
  26.5 1.4 %correlate.7 = (f32[2,8,64,128]{3,2,1,0:T(8,128)S(1)}, f32[8,64,1024]{2,1,0:T(8,128)}) custom-call(bf16[512,1536]{1,0:T(8,128)(2,1)S(1)} %modulate.1.modulated, bf16[64,1536]{1,0:T(8,128)(2,1)S(1)} %collective-permute-done.1.rest_0_, bf16[64,1536]{1,0:T(8,128)(2,1)S(1)} %collective-permute-done.7.rest_1_, ...), custom_call_target="tpu_custom_call", output_to_operand_aliasing={{1}: (6, {})} | custom-call | flops 402653184 | tf_op jit(solution)/shard_map/correlate/pallas_call | solution.py:201
  27.8 1.3 %correlate.8 = (f32[2,8,64,128]{3,2,1,0:T(8,128)S(1)}, f32[8,64,1024]{2,1,0:T(8,128)}) custom-call(bf16[512,1536]{1,0:T(8,128)(2,1)S(1)} %modulate.1.modulated, bf16[64,1536]{1,0:T(8,128)(2,1)S(1)} %collective-permute-done.8.rest_0_, bf16[64,1536]{1,0:T(8,128)(2,1)S(1)} %collective-permute-done.2.rest_1_, ...), custom_call_target="tpu_custom_call", output_to_operand_aliasing={{1}: (6, {})} | custom-call | flops 402653184 | tf_op jit(solution)/shard_map/correlate/pallas_call | solution.py:201
  29.1 1.3 %correlate.9 = f32[8,64,1024]{2,1,0:T(8,128)} custom-call(bf16[512,1536]{1,0:T(8,128)(2,1)S(1)} %modulate.1.modulated, bf16[64,1536]{1,0:T(8,128)(2,1)S(1)} %collective-permute-done.3.rest_0_, bf16[64,1536]{1,0:T(8,128)(2,1)S(1)} %collective-permute-done.4.rest_1_, f32[2,8,64,128]{3,2,1,0:T(8,128)S(1)} %get-tuple-element.19.rest_2_, ...), custom_call_target="tpu_custom_call", output_to_operand_aliasing={{}: (4, {})} | custom-call | flops 201326592 | tf_op jit(solution)/shard_map/correlate/pallas_call | solution.py:201
  (13 shorter events, 0.1 us)
Async XLA Ops:
  1.3 3.2 %collective-permute-start.5 = (bf16[64,1536]{1,0:T(8,128)(2,1)S(1)}, bf16[64,1536]{1,0:T(8,128)(2,1)S(1)}, u32[]{:S(2)}, u32[]{:S(2)}) collective-permute-start(bf16[64,1536]{1,0:T(8,128)(2,1)S(1)} %get-tuple-element.13.white.rest_0_), channel_id=1, source_target_pairs={{0,1},{1,0},{2,3},{3,2},{4,5},{5,4},{6,7},{7,6},{8,9},{9,8},{10,11... | collective-permute-start | bytes 589832 | tf_op jit(solution)/shard_map/ppermute | solution.py:240
  1.9 6.0 %collective-permute-start = (bf16[64,1536]{1,0:T(8,128)(2,1)S(1)}, bf16[64,1536]{1,0:T(8,128)(2,1)S(1)}, u32[]{:S(2)}, u32[]{:S(2)}) collective-permute-start(bf16[64,1536]{1,0:T(8,128)(2,1)S(1)} %get-tuple-element.13.white.rest_0_), channel_id=1, source_target_pairs={{0,5},{1,2},{4,9},{5,0},{8,13},{9,4},{12,15},{13,8},{14,11},{15,12... | collective-permute-start | bytes 589832 | tf_op jit(solution)/shard_map/ppermute | solution.py:237
  4.6 5.5 %collective-permute-start.6 = (bf16[64,1536]{1,0:T(8,128)(2,1)S(1)}, bf16[64,1536]{1,0:T(8,128)(2,1)S(1)}, u32[]{:S(2)}, u32[]{:S(2)}) collective-permute-start(bf16[64,1536]{1,0:T(8,128)(2,1)S(1)} %collective-permute-done.5.rest_1_), channel_id=1, source_target_pairs={{0,5},{1,2},{4,9},{5,0},{8,13},{9,4},{12,15},{13,8},{14,11},{15,12... | collective-permute-start | bytes 589832 | tf_op jit(solution)/shard_map/ppermute | solution.py:237
  7.9 5.3 %collective-permute-start.1 = (bf16[64,1536]{1,0:T(8,128)(2,1)S(1)}, bf16[64,1536]{1,0:T(8,128)(2,1)S(1)}, u32[]{:S(2)}, u32[]{:S(2)}) collective-permute-start(bf16[64,1536]{1,0:T(8,128)(2,1)S(1)} %collective-permute-done.rest_1_), channel_id=1, source_target_pairs={{1,4},{0,3},{5,8},{4,1},{9,12},{8,5},{13,14},{12,9},{15,10},{14,13... | collective-permute-start | bytes 589832 | tf_op jit(solution)/shard_map/ppermute | solution.py:237
  10.0 5.8 %collective-permute-start.7 = (bf16[64,1536]{1,0:T(8,128)(2,1)S(1)}, bf16[64,1536]{1,0:T(8,128)(2,1)S(1)}, u32[]{:S(2)}, u32[]{:S(2)}) collective-permute-start(bf16[64,1536]{1,0:T(8,128)(2,1)S(1)} %collective-permute-done.6.rest_0_), channel_id=1, source_target_pairs={{1,4},{0,3},{5,8},{4,1},{9,12},{8,5},{13,14},{12,9},{15,10},{14,13... | collective-permute-start | bytes 589832 | tf_op jit(solution)/shard_map/ppermute | solution.py:237
  13.2 5.4 %collective-permute-start.2 = (bf16[64,1536]{1,0:T(8,128)(2,1)S(1)}, bf16[64,1536]{1,0:T(8,128)(2,1)S(1)}, u32[]{:S(2)}, u32[]{:S(2)}) collective-permute-start(bf16[64,1536]{1,0:T(8,128)(2,1)S(1)} %collective-permute-done.1.rest_0_), channel_id=1, source_target_pairs={{0,5},{1,2},{4,9},{5,0},{8,13},{9,4},{12,15},{13,8},{14,11},{15,12... | collective-permute-start | bytes 589832 | tf_op jit(solution)/shard_map/ppermute | solution.py:237
  15.3 5.3 %collective-permute-start.13 = (bf16[64,1536]{1,0:T(8,128)(2,1)S(1)}, bf16[64,1536]{1,0:T(8,128)(2,1)S(1)}, u32[]{:S(2)}, u32[]{:S(2)}) collective-permute-start(bf16[64,1536]{1,0:T(8,128)(2,1)S(1)} %collective-permute-done.rest_1_), channel_id=1, source_target_pairs={{0,1},{1,0},{2,3},{3,2},{4,5},{5,4},{6,7},{7,6},{8,9},{9,8},{10,11... | collective-permute-start | bytes 589832 | tf_op jit(solution)/shard_map/ppermute | solution.py:240
  15.3 5.8 %collective-permute-start.14 = (bf16[64,1536]{1,0:T(8,128)(2,1)S(1)}, bf16[64,1536]{1,0:T(8,128)(2,1)S(1)}, u32[]{:S(2)}, u32[]{:S(2)}) collective-permute-start(bf16[64,1536]{1,0:T(8,128)(2,1)S(1)} %collective-permute-done.6.rest_0_), channel_id=1, source_target_pairs={{0,1},{1,0},{2,3},{3,2},{4,5},{5,4},{6,7},{7,6},{8,9},{9,8},{10,11... | collective-permute-start | bytes 589832 | tf_op jit(solution)/shard_map/ppermute | solution.py:240
  15.8 5.4 %collective-permute-start.8 = (bf16[64,1536]{1,0:T(8,128)(2,1)S(1)}, bf16[64,1536]{1,0:T(8,128)(2,1)S(1)}, u32[]{:S(2)}, u32[]{:S(2)}) collective-permute-start(bf16[64,1536]{1,0:T(8,128)(2,1)S(1)} %collective-permute-done.7.rest_1_), channel_id=1, source_target_pairs={{0,5},{1,2},{4,9},{5,0},{8,13},{9,4},{12,15},{13,8},{14,11},{15,12... | collective-permute-start | bytes 589832 | tf_op jit(solution)/shard_map/ppermute | solution.py:237
  18.7 5.3 %collective-permute-start.3 = (bf16[64,1536]{1,0:T(8,128)(2,1)S(1)}, bf16[64,1536]{1,0:T(8,128)(2,1)S(1)}, u32[]{:S(2)}, u32[]{:S(2)}) collective-permute-start(bf16[64,1536]{1,0:T(8,128)(2,1)S(1)} %collective-permute-done.2.rest_1_), channel_id=1, source_target_pairs={{1,4},{0,3},{5,8},{4,1},{9,12},{8,5},{13,14},{12,9},{15,10},{14,13... | collective-permute-start | bytes 589832 | tf_op jit(solution)/shard_map/ppermute | solution.py:237
  20.7 5.8 %collective-permute-start.12 = (bf16[64,1536]{1,0:T(8,128)(2,1)S(1)}, bf16[64,1536]{1,0:T(8,128)(2,1)S(1)}, u32[]{:S(2)}, u32[]{:S(2)}) collective-permute-start(bf16[64,1536]{1,0:T(8,128)(2,1)S(1)} %collective-permute-done.1.rest_0_), channel_id=1, source_target_pairs={{0,1},{1,0},{2,3},{3,2},{4,5},{5,4},{6,7},{7,6},{8,9},{9,8},{10,11... | collective-permute-start | bytes 589832 | tf_op jit(solution)/shard_map/ppermute | solution.py:240
  20.7 5.8 %collective-permute-start.11 = (bf16[64,1536]{1,0:T(8,128)(2,1)S(1)}, bf16[64,1536]{1,0:T(8,128)(2,1)S(1)}, u32[]{:S(2)}, u32[]{:S(2)}) collective-permute-start(bf16[64,1536]{1,0:T(8,128)(2,1)S(1)} %collective-permute-done.7.rest_1_), channel_id=1, source_target_pairs={{0,1},{1,0},{2,3},{3,2},{4,5},{5,4},{6,7},{7,6},{8,9},{9,8},{10,11... | collective-permute-start | bytes 589832 | tf_op jit(solution)/shard_map/ppermute | solution.py:240
  21.2 6.6 %collective-permute-start.9 = (bf16[64,1536]{1,0:T(8,128)(2,1)S(1)}, bf16[64,1536]{1,0:T(8,128)(2,1)S(1)}, u32[]{:S(2)}, u32[]{:S(2)}) collective-permute-start(bf16[64,1536]{1,0:T(8,128)(2,1)S(1)} %collective-permute-done.2.rest_1_), channel_id=1, source_target_pairs={{0,1},{1,0},{2,3},{3,2},{4,5},{5,4},{6,7},{7,6},{8,9},{9,8},{10,11... | collective-permute-start | bytes 589832 | tf_op jit(solution)/shard_map/ppermute | solution.py:240
  21.3 6.6 %collective-permute-start.10 = (bf16[64,1536]{1,0:T(8,128)(2,1)S(1)}, bf16[64,1536]{1,0:T(8,128)(2,1)S(1)}, u32[]{:S(2)}, u32[]{:S(2)}) collective-permute-start(bf16[64,1536]{1,0:T(8,128)(2,1)S(1)} %collective-permute-done.8.rest_0_), channel_id=1, source_target_pairs={{0,1},{1,0},{2,3},{3,2},{4,5},{5,4},{6,7},{7,6},{8,9},{9,8},{10,11... | collective-permute-start | bytes 589832 | tf_op jit(solution)/shard_map/ppermute | solution.py:240
  24.0 5.1 %collective-permute-start.4 = (bf16[64,1536]{1,0:T(8,128)(2,1)S(1)}, bf16[64,1536]{1,0:T(8,128)(2,1)S(1)}, u32[]{:S(2)}, u32[]{:S(2)}) collective-permute-start(bf16[64,1536]{1,0:T(8,128)(2,1)S(1)} %collective-permute-done.3.rest_0_), channel_id=1, source_target_pairs={{0,1},{1,0},{2,3},{3,2},{4,5},{5,4},{6,7},{7,6},{8,9},{9,8},{10,11... | collective-permute-start | bytes 589832 | tf_op jit(solution)/shard_map/ppermute | solution.py:240
